TPU v7x, 32 devices: a whole 2x2x4 slice. The times are simulated.
32 devices in a mesh: dp: 8 (over z, x), seq: 4 (over y, core).
Axes of the slice: x: 2, y: 2, z: 4, core: 2. Of those that a mesh axis runs over, the one named last changes fastest.
Arguments:
- short_input: bfloat16 [192, 128, 1024], P(('dp', 'seq')), may hold values from -6 to 6
- long_input: bfloat16 [16, 512, 1024], P('dp', 'seq'), may hold values from -6 to 6
- short_cotangent: bfloat16 [192, 128, 1024], P(('dp', 'seq')), may hold values from -6 to 6
- long_cotangent: bfloat16 [16, 512, 1024], P('dp', 'seq'), may hold values from -6 to 6
- short_lengths: int32 [192], P(('dp', 'seq')), may hold values from 32 to 128, as said below
- long_lengths: int32 [16], P('dp'), may hold values from 128 to 512, as said below
- query_weight: float32 [1024, 1024], P(('dp', 'seq')), may hold values from -0.1875 to 0.1875
- key_weight: float32 [1024, 1024], P(('dp', 'seq')), may hold values from -0.1875 to 0.1875
- value_weight: float32 [1024, 1024], P(('dp', 'seq')), may hold values from -0.1875 to 0.1875
- output_weight: float32 [1024, 1024], P(('dp', 'seq')), may hold values from -0.75 to 0.75
- upward_weight: float32 [1024, 4096], P(('dp', 'seq')), may hold values from -0.1875 to 0.1875
- downward_weight: float32 [4096, 1024], P(('dp', 'seq')), may hold values from -0.09375 to 0.09375
- query_bias: float32 [1024], replicated, may hold values from -3 to 3
- value_bias: float32 [1024], replicated, may hold values from -3 to 3
- output_bias: float32 [1024], replicated, may hold values from -3 to 3
- upward_bias: float32 [4096], replicated, may hold values from -3 to 3
- downward_bias: float32 [1024], replicated, may hold values from -3 to 3
- first_gain: float32 [1024], replicated, may hold values from 0.25 to 1.75
- first_shift: float32 [1024], replicated, may hold values from -3 to 3
- second_gain: float32 [1024], replicated, may hold values from 0.25 to 1.75
- second_shift: float32 [1024], replicated, may hold values from -3 to 3
Outputs:
- short_output: bfloat16 [192, 128, 1024], P(('dp', 'seq'))
- long_output: bfloat16 [16, 512, 1024], P('dp', 'seq')
- short_grad: bfloat16 [192, 128, 1024], P(('dp', 'seq'))
- long_grad: bfloat16 [16, 512, 1024], P('dp', 'seq')
- query_delta: float32 [1024], replicated
- value_delta: float32 [1024], replicated
- output_delta: float32 [1024], replicated
- upward_delta: float32 [4096], replicated
- downward_delta: float32 [1024], replicated
- first_delta: float32 [1024], replicated
- second_delta: float32 [1024], replicated
Inputs may be any that keep to these rules, and one draw needn't show every extreme that they name: `short_lengths`: some short sequence has all 128 positions. `long_lengths`: some long sequence has all 512 positions.
All inputs are finite; a program needn't handle non-finite values.
Results may differ from a plain program's by a relative error of at most 0.013.
The roundings to bfloat16 on the way count: a program that leaves them out, or rounds other values in their place, can miss the bound.
Values may be sent and summed in bfloat16 or wider, within the bound.
A program may use at most 192 MiB of HBM per device.

v0:
```python
import jax
import jax.numpy as jnp
from jax import lax
from jax.sharding import PartitionSpec as P

HEADS = 16
HEAD = 64


epsilon = 1e-12
masked = -1e30


def forward_product(left, right):
    return jnp.dot(left, right, preferred_element_type=jnp.float32)


def backward_product(left, right):
    return lax.dot_general(
        left, right, (((left.ndim - 1,), (1,)), ((), ())), preferred_element_type=jnp.float32
    )


def exact_backward(left, right):
    return lax.dot_general(
        left,
        right,
        (((left.ndim - 1,), (1,)), ((), ())),
        precision=lax.Precision.HIGHEST,
        preferred_element_type=jnp.float32,
    )


def norm_apply(value, gain, shift):
    center = value - jnp.mean(value, axis=-1, keepdims=True)
    spread = jnp.mean(center * center, axis=-1, keepdims=True)
    return center * lax.rsqrt(spread + epsilon) * gain + shift


def token_total(value):
    return jnp.sum(value, axis=(0, 1))


def keep_local(first_part, second_part):
    return (first_part, second_part)


def spread_long(key_rows, values):
    return (
        lax.all_gather(key_rows, "seq", axis=1, tiled=True),
        lax.all_gather(values, "seq", axis=1, tiled=True),
    )


def settle_each(value):
    return lax.psum(value, ("dp", "seq"))


def finish_local(key_terms, value_terms, key_exact, value_exact, settle):
    value_delta = settle(token_total(value_terms))
    through = exact_backward(key_terms, key_exact) + exact_backward(value_terms, value_exact)
    return (through, value_delta)


def finish_summed(key_terms, value_terms, key_exact, value_exact, settle):
    key_grad, value_grad = (
        lax.psum_scatter(
            key_terms.astype(jnp.bfloat16), "seq", scatter_dimension=1, tiled=True
        ).astype(jnp.float32),
        lax.psum_scatter(
            value_terms.astype(jnp.bfloat16), "seq", scatter_dimension=1, tiled=True
        ).astype(jnp.float32),
    )
    value_delta = settle(token_total(value_grad))
    through = exact_backward(key_grad, key_exact) + exact_backward(value_grad, value_exact)
    return (through, value_delta)


def recompute(inputs, usable, weights, params, spread):
    query_weight, key_weight, value_weight, output_weight, upward_weight, downward_weight = weights
    (
        query_bias,
        value_bias,
        output_bias,
        upward_bias,
        downward_bias,
        first_gain,
        first_shift,
        second_gain,
        second_shift,
    ) = params
    number, seqlen, breadth = inputs.shape
    queries = (forward_product(inputs, query_weight) + query_bias).astype(jnp.bfloat16)
    key_rows = forward_product(inputs, key_weight).astype(jnp.bfloat16)
    values = (forward_product(inputs, value_weight) + value_bias).astype(jnp.bfloat16)
    key_all, value_all = spread(key_rows, values)
    query_heads = queries.reshape(number, seqlen, HEADS, HEAD)
    key_heads = key_all.reshape(number, key_all.shape[1], HEADS, HEAD)
    value_heads = value_all.reshape(number, value_all.shape[1], HEADS, HEAD)
    scores = jnp.einsum(
        "nqhd,nkhd->nhqk", query_heads, key_heads, preferred_element_type=jnp.float32
    ) * HEAD ** (-0.5)
    scores = jnp.where(usable[:, None, None, :], scores, masked)
    attention = jax.nn.softmax(scores, axis=-1)
    attention_low = attention.astype(jnp.bfloat16)
    blended = jnp.einsum(
        "nhqk,nkhd->nqhd", attention_low, value_heads, preferred_element_type=jnp.float32
    )
    blended = blended.reshape(number, seqlen, breadth).astype(jnp.bfloat16)
    residual = inputs.astype(jnp.float32) + forward_product(blended, output_weight) + output_bias
    normed = norm_apply(residual, first_gain, first_shift)
    pre_up = forward_product(normed.astype(jnp.bfloat16), upward_weight) + upward_bias
    active = jax.nn.gelu(pre_up, approximate=True).astype(jnp.bfloat16)
    ffn_sum = normed + forward_product(active, downward_weight) + downward_bias
    output = norm_apply(ffn_sum, second_gain, second_shift)
    return (
        query_heads,
        key_heads,
        value_heads,
        attention,
        attention_low,
        residual,
        pre_up,
        ffn_sum,
        output,
    )


def backprop(inputs, cotangent, usable, weights, params, spread, finish, settle):
    (
        query_heads,
        key_heads,
        value_heads,
        attention,
        attention_low,
        residual,
        pre_up,
        ffn_sum,
        output,
    ) = recompute(inputs, usable, weights, params, spread)
    query_weight, key_weight, value_weight, output_weight, upward_weight, downward_weight = weights
    (
        query_bias,
        value_bias,
        output_bias,
        upward_bias,
        downward_bias,
        first_gain,
        first_shift,
        second_gain,
        second_shift,
    ) = params
    number, seqlen, breadth = inputs.shape
    upstream = cotangent.astype(jnp.float32)
    second_pull = jax.vjp(lambda value: norm_apply(value, second_gain, second_shift), ffn_sum)[1]
    ffn_grad = second_pull(upstream)[0]
    second_delta = settle(token_total(upstream))
    downward_delta = settle(token_total(ffn_grad))
    active_grad = backward_product(ffn_grad.astype(jnp.bfloat16), downward_weight)
    gelu_pull = jax.vjp(lambda value: jax.nn.gelu(value, approximate=True), pre_up)[1]
    pre_grad = gelu_pull(active_grad)[0]
    upward_delta = settle(token_total(pre_grad))
    normed_grad = ffn_grad + backward_product(pre_grad.astype(jnp.bfloat16), upward_weight)
    first_delta = settle(token_total(normed_grad))
    first_pull = jax.vjp(lambda value: norm_apply(value, first_gain, first_shift), residual)[1]
    residual_grad = first_pull(normed_grad)[0]
    output_delta = settle(token_total(residual_grad))
    blended_grad = backward_product(residual_grad.astype(jnp.bfloat16), output_weight).astype(
        jnp.bfloat16
    )
    blended_grad = blended_grad.reshape(number, seqlen, HEADS, HEAD)
    prob_grad = jnp.einsum(
        "nqhd,nkhd->nhqk", blended_grad, value_heads, preferred_element_type=jnp.float32
    )
    score_grad = attention * (prob_grad - jnp.sum(prob_grad * attention, axis=-1, keepdims=True))
    score_grad = score_grad.astype(jnp.bfloat16)
    query_grad = jnp.einsum(
        "nhqk,nkhd->nqhd", score_grad, key_heads, preferred_element_type=jnp.float32
    )
    query_grad = query_grad.reshape(number, seqlen, breadth) * HEAD ** (-0.5)
    key_terms = jnp.einsum(
        "nhqk,nqhd->nkhd", score_grad, query_heads, preferred_element_type=jnp.float32
    )
    key_terms = key_terms.reshape(number, key_heads.shape[1], breadth) * HEAD ** (-0.5)
    value_terms = jnp.einsum(
        "nhqk,nqhd->nkhd", attention_low, blended_grad, preferred_element_type=jnp.float32
    )
    value_terms = value_terms.reshape(number, value_heads.shape[1], breadth)
    key_exact = key_weight.astype(jnp.float32)
    value_exact = value_weight.astype(jnp.float32)
    through, value_delta = finish(key_terms, value_terms, key_exact, value_exact, settle)
    query_delta = settle(token_total(query_grad))
    input_grad = (
        residual_grad + backward_product(query_grad.astype(jnp.bfloat16), query_weight) + through
    )
    deltas = (
        query_delta,
        value_delta,
        output_delta,
        upward_delta,
        downward_delta,
        first_delta,
        second_delta,
    )
    return (input_grad.astype(jnp.bfloat16), deltas)


def on_device(
    short_input,
    long_input,
    short_cotangent,
    long_cotangent,
    short_lengths,
    long_lengths,
    query_weight,
    key_weight,
    value_weight,
    output_weight,
    upward_weight,
    downward_weight,
    query_bias,
    value_bias,
    output_bias,
    upward_bias,
    downward_bias,
    first_gain,
    first_shift,
    second_gain,
    second_shift,
):
    params = (
        query_bias,
        value_bias,
        output_bias,
        upward_bias,
        downward_bias,
        first_gain,
        first_shift,
        second_gain,
        second_shift,
    )
    short_usable = jnp.arange(short_input.shape[1])[None, :] < short_lengths[:, None]
    long_span = long_input.shape[1] * lax.axis_size("seq")
    long_usable = jnp.arange(long_span)[None, :] < long_lengths[:, None]
    query_low = query_weight.astype(jnp.bfloat16)
    key_low = key_weight.astype(jnp.bfloat16)
    value_low = value_weight.astype(jnp.bfloat16)
    output_low = output_weight.astype(jnp.bfloat16)
    upward_low = upward_weight.astype(jnp.bfloat16)
    downward_low = downward_weight.astype(jnp.bfloat16)
    gathered = (
        lax.all_gather(query_low, ("dp", "seq"), axis=0, tiled=True),
        lax.all_gather(key_low, ("dp", "seq"), axis=0, tiled=True),
        lax.all_gather(value_low, ("dp", "seq"), axis=0, tiled=True),
        lax.all_gather(output_low, ("dp", "seq"), axis=0, tiled=True),
        lax.all_gather(upward_low, ("dp", "seq"), axis=0, tiled=True),
        lax.all_gather(downward_low, ("dp", "seq"), axis=0, tiled=True),
    )
    short_output = recompute(short_input, short_usable, gathered, params, keep_local)[-1]
    long_output = recompute(long_input, long_usable, gathered, params, spread_long)[-1]
    regathered = (
        lax.all_gather(query_low, ("dp", "seq"), axis=0, tiled=True),
        lax.all_gather(key_low, ("dp", "seq"), axis=0, tiled=True),
        lax.all_gather(value_low, ("dp", "seq"), axis=0, tiled=True),
        lax.all_gather(output_low, ("dp", "seq"), axis=0, tiled=True),
        lax.all_gather(upward_low, ("dp", "seq"), axis=0, tiled=True),
        lax.all_gather(downward_low, ("dp", "seq"), axis=0, tiled=True),
    )
    short_grad, short_deltas = backprop(
        short_input,
        short_cotangent,
        short_usable,
        regathered,
        params,
        keep_local,
        finish_local,
        settle_each,
    )
    long_grad, long_deltas = backprop(
        long_input,
        long_cotangent,
        long_usable,
        regathered,
        params,
        spread_long,
        finish_summed,
        settle_each,
    )
    summed = tuple(
        (first_part + second_part for first_part, second_part in zip(short_deltas, long_deltas))
    )
    return (
        short_output.astype(jnp.bfloat16),
        long_output.astype(jnp.bfloat16),
        short_grad,
        long_grad,
        summed[0],
        summed[1],
        summed[2],
        summed[3],
        summed[4],
        summed[5],
        summed[6],
    )


def solution(mesh):
    placed = (
        P(("dp", "seq"), None, None),
        P("dp", "seq", None),
        P(("dp", "seq"), None, None),
        P("dp", "seq", None),
        P(("dp", "seq")),
        P("dp"),
        P(("dp", "seq"), None),
        P(("dp", "seq"), None),
        P(("dp", "seq"), None),
        P(("dp", "seq"), None),
        P(("dp", "seq"), None),
        P(("dp", "seq"), None),
        P(),
        P(),
        P(),
        P(),
        P(),
        P(),
        P(),
        P(),
        P(),
    )
    return jax.shard_map(
        on_device,
        mesh=mesh,
        in_specs=placed,
        out_specs=(
            P(("dp", "seq"), None, None),
            P("dp", "seq", None),
            P(("dp", "seq"), None, None),
            P("dp", "seq", None),
            P(),
            P(),
            P(),
            P(),
            P(),
            P(),
            P(),
        ),
        check_vma=False,
    )
```

profile of v0, /device:TPU:0, one launch (start us, length us, event | category | flops | bytes accessed | tf_op | source)
XLA Modules:
  0.0 694.6 jit_solution(11124600776407439953)
XLA Ops:
  13.7 56.7 %all-gather.9.cloned.1.call-done = bf16[1024,1024]{1,0:T(8,128)(2,1)} async-done(((bf16[32,1024]{1,0:T(8,128)(2,1)}), bf16[1024,1024]{1,0:T(8,128)(2,1)}) %all-gather.9.cloned.1.call-update) | async-done | bytes 2097168 | tf_op jit(solution)/shard_map/all_gather | solution.py:254
  73.7 55.3 %all-gather.13.cloned.1.call-done = bf16[1024,1024]{1,0:T(8,128)(2,1)} async-done(((bf16[32,1024]{1,0:T(8,128)(2,1)}), bf16[1024,1024]{1,0:T(8,128)(2,1)}) %all-gather.13.cloned.1.call-update) | async-done | bytes 2097168 | tf_op jit(solution)/shard_map/all_gather | solution.py:253
  134.0 53.6 %all-gather.11.cloned.1.call-done = bf16[1024,1024]{1,0:T(8,128)(2,1)} async-done(((bf16[32,1024]{1,0:T(8,128)(2,1)}), bf16[1024,1024]{1,0:T(8,128)(2,1)}) %all-gather.11.cloned.1.call-update) | async-done | bytes 2097168 | tf_op jit(solution)/shard_map/all_gather | solution.py:252
  219.2 26.2 %all-gather.15.cloned.1.call-done = bf16[1024,1024]{1,0:T(8,128)(2,1)} async-done(((bf16[32,1024]{1,0:T(8,128)(2,1)}), bf16[1024,1024]{1,0:T(8,128)(2,1)}) %all-gather.15.cloned.1.call-update) | async-done | bytes 2097168 | tf_op jit(solution)/shard_map/all_gather | solution.py:255
  251.0 17.8 %all-gather.21.cloned.1.call-done = bf16[2,512,1024]{2,1,0:T(8,128)(2,1)} async-done(((bf16[2,128,1024]{2,1,0:T(8,128)(2,1)}), bf16[2,512,1024]{2,1,0:T(8,128)(2,1)}) %all-gather.21.cloned.1.call-update) | async-done | bytes 2097168 | tf_op jit(solution)/shard_map/all_gather | solution.py:51
  272.8 20.0 %all-gather.23.cloned.1.call-done = bf16[2,512,1024]{2,1,0:T(8,128)(2,1)} async-done(((bf16[2,128,1024]{2,1,0:T(8,128)(2,1)}), bf16[2,512,1024]{2,1,0:T(8,128)(2,1)}) %all-gather.23.cloned.1.call-update) | async-done | bytes 2097168 | tf_op jit(solution)/shard_map/all_gather | solution.py:50
  297.1 7.9 %fusion.219 = (f32[2,16,128]{2,1,0:T(8,128)S(1)}, f32[2,16,128,512]{3,2,1,0:T(8,128)}) fusion(pred[2,512]{1,0:T(4,128)(4,1)S(1)} %iota_compare_fusion, bf16[2,128,16,64]{1,3,2,0:T(8,128)(2,1)} %bitcast.210, bf16[2,512,16,64]{1,3,2,0:T(8,128)(2,1)} %bitcast.198), kind=kOutput, calls=%fused_computation.229 | convolution fusion | flops 276824576 | bytes 11027456 | tf_op jit(solution)/shard_map/sub | solution.py:104
  312.9 59.9 %all-gather.17.cloned.1.call-done = bf16[1024,4096]{1,0:T(8,128)(2,1)} async-done(((bf16[32,4096]{1,0:T(8,128)(2,1)}), bf16[1024,4096]{1,0:T(8,128)(2,1)}) %all-gather.17.cloned.1.call-update) | async-done | bytes 8388624 | tf_op jit(solution)/shard_map/all_gather | solution.py:256
  372.8 8.1 %fusion.30 = f32[2,128,4096]{2,1,0:T(8,128)} fusion(bf16[1024,4096]{1,0:T(8,128)(2,1)} %all-gather.17.cloned.1.call-done, f32[4096]{0:T(1024)S(1)} %copy-done.49, f32[2,128,1024]{2,1,0:T(8,128)} %copy-done.11, f32[1024]{0:T(1024)S(1)} %copy-done.53, f32[1024]{0:T(1024)S(1)} %copy-done.46, f32[2,128]{1,0:T(2,128)S(1)} %fusion.195, ...), kind=kOutput, calls=%fused_computation.43 | convolution fusion | flops 2149842944 | bytes 13658112 | tf_op jit(solution)/shard_map/dot_general | solution.py:15
  380.9 70.5 %all-gather.19.cloned.1.call-done = bf16[4096,1024]{1,0:T(8,128)(2,1)} async-done(((bf16[128,1024]{1,0:T(8,128)(2,1)}), bf16[4096,1024]{1,0:T(8,128)(2,1)}) %all-gather.19.cloned.1.call-update) | async-done | bytes 8388624 | tf_op jit(solution)/shard_map/all_gather | solution.py:257
  451.4 7.8 %fusion.221 = (f32[2,128]{1,0:T(2,128)S(1)}, f32[2,128,1024]{2,1,0:T(8,128)S(1)}) fusion(f32[1024]{0:T(1024)S(1)} %copy-done.52, bf16[4096,1024]{1,0:T(8,128)(2,1)} %all-gather.19.cloned.1.call-done, f32[2,128,4096]{2,1,0:T(8,128)} %fusion.30, f32[1024]{0:T(1024)S(1)} %copy-done.53, f32[1024]{0:T(1024)S(1)} %copy-done.46, f32[2,128]{1,0:T(2,128)S(1)} %fusion.195, ...), kind=kOutput, calls=%fused_computation.231 | convolution fusion | flops 2158755584 | bytes 14695424 | tf_op jit(solution)/shard_map/dot_general | solution.py:15
  460.1 8.3 %fusion.223 = (f32[4096]{0:T(1024)S(1)}, bf16[2,128,4096]{2,1,0:T(8,128)(2,1)S(1)}) fusion(f32[2,128,4096]{2,1,0:T(8,128)S(1)} %copy-done.56, bf16[4096,1024]{1,0:T(8,128)(2,1)} %all-gather.19.cloned.1.call-done, f32[2,128]{1,0:T(2,128)S(1)} %negate_multiply_fusion.3, f32[2,128]{1,0:T(2,128)S(1)} %get-tuple-element.42, ...), kind=kOutput, calls=%fused_computation.233 | convolution fusion | flops 2171858944 | bytes 16277504 | tf_op jit(solution)/shard_map/dot_general | solution.py:19
  476.9 5.9 fusion.95
  482.8 6.5 multiply_reduce_fusion
  493.3 13.0 %fusion.22 = f32[6,128,4096]{2,1,0:T(8,128)} fusion(bf16[1024,4096]{1,0:T(8,128)(2,1)} %all-gather.17.cloned.1.call-done, f32[6,128,1024]{2,1,0:T(8,128)S(1)} %get-tuple-element.47, f32[1024]{0:T(1024)S(1)} %copy-done.53, f32[1024]{0:T(1024)S(1)} %copy-done.46, f32[6,128]{1,0:T(8,128)S(1)} %fusion.193, f32[6,128]{1,0:T(8,128)S(1)} %broadcast_multiply_fusion.1), kind=kOutput, calls=%fused_computation.25 | convolution fusion | flops 6446383104 | bytes 24131584 | tf_op jit(solution)/shard_map/dot_general | solution.py:15
  506.3 14.4 %fusion.218 = (f32[6,128]{1,0:T(8,128)S(1)}, f32[6,128,1024]{2,1,0:T(8,128)S(1)}) fusion(f32[1024]{0:T(1024)S(1)} %copy-done.52, bf16[4096,1024]{1,0:T(8,128)(2,1)} %all-gather.19.cloned.1.call-done, f32[6,128,4096]{2,1,0:T(8,128)} %fusion.22, f32[4096]{0:T(1024)S(1)} %copy-done.49, f32[1024]{0:T(1024)S(1)} %copy-done.53, f32[1024]{0:T(1024)S(1)} %copy-done.46, ...), kind=kOutput, calls=%fused_computation.228 | convolution fusion | flops 6479412224 | bytes 27300864 | tf_op jit(solution)/shard_map/dot_general | solution.py:15
  527.0 22.6 %fusion.222 = (f32[4096]{0:T(1024)S(1)}, bf16[6,128,4096]{2,1,0:T(8,128)(2,1)}) fusion(f32[6,128,4096]{2,1,0:T(8,128)} %fusion.22, f32[4096]{0:T(1024)S(1)} %copy-done.49, bf16[4096,1024]{1,0:T(8,128)(2,1)} %all-gather.19.cloned.1.call-done, f32[6,128]{1,0:T(8,128)S(1)} %negate_multiply_fusion.1, f32[6,128]{1,0:T(8,128)S(1)} %get-tuple-element.40, ...), kind=kOutput, calls=%fused_computation.232 | convolution fusion | flops 6518730752 | bytes 32030720 | tf_op jit(solution)/shard_map/dot_general | solution.py:19
  549.7 13.8 %fusion.211 = (f32[1024]{0:T(1024)S(1)}, f32[6,128]{1,0:T(8,128)S(1)}, f32[6,128,1024]{2,1,0:T(8,128)}) fusion(f32[1024]{0:T(1024)S(1)} %copy-done.46, f32[6,128,1024]{2,1,0:T(8,128)S(1)} %get-tuple-element.47, f32[6,128]{1,0:T(8,128)S(1)} %broadcast_multiply_fusion.1, bf16[1024,4096]{1,0:T(8,128)(2,1)} %all-gather.17.cloned.1.call-done, ...), kind=kOutput, calls=%fused_computation.221 | convolution fusion | flops 6453458944 | bytes 25720832 | tf_op jit(solution)/shard_map/dot_general | solution.py:19
  577.9 7.3 %bitcast_reduce_fusion = (f32[16,64]{1,0:T(8,128)S(1)}, f32[6,16,64,128]{3,2,1,0:T(8,128)}) fusion(bf16[6,128,16,64]{1,3,2,0:T(8,128)(2,1)} %bitcast.214, f32[6,16,128,128]{2,3,1,0:T(8,128)} %get-tuple-element.45, f32[6,16,128]{2,1,0:T(8,128)S(1)} %copy-done.43), kind=kOutput, calls=%fused_computation.64 | convolution fusion | flops 205257728 | bytes 11063296 | tf_op jit(solution)/shard_map/nhqk,nqhd->nkhd/dot_general | solution.py:185
  590.0 6.9 multiply_reduce_fusion.1
  596.9 7.0 %multiply_convert_fusion.2 = bf16[6,16,128,128]{2,3,1,0:T(8,128)(2,1)S(1)} fusion(f32[6,16,128,128]{2,3,1,0:T(8,128)} %get-tuple-element.58, f32[6,16,128]{2,1,0:T(8,128)S(1)} %get-tuple-element.57, f32[6,16,128,128]{2,3,1,0:T(8,128)} %get-tuple-element.45, f32[6,16,128]{2,1,0:T(8,128)S(1)} %copy-done.43), kind=kLoop, calls=%fused_computation.32 | loop fusion | flops 6291456 | bytes 15826944 | tf_op jit(solution)/shard_map/convert_element_type | solution.py:176
  617.9 10.3 %fusion.80 = f32[6,128,1024]{2,1,0:T(8,128)S(1)} fusion(f32[6,128,1024]{1,2,0:T(8,128)S(1)} %bitcast.222, bf16[1024,1024]{1,0:T(8,128)(2,1)S(1)} %copy-done.27), kind=kOutput, calls=%fused_computation.113 | convolution fusion | flops 9663676416 | bytes 8388608 | tf_op jit(solution)/shard_map/dot_general | solution.py:25
  628.2 10.2 %fusion.64 = f32[6,128,1024]{2,1,0:T(8,128)S(1)} fusion(f32[6,128,1024]{1,2,0:T(8,128)S(1)} %bitcast.204, bf16[1024,1024]{1,0:T(8,128)(2,1)S(1)} %copy-done.24), kind=kOutput, calls=%fused_computation.97 | convolution fusion | flops 9663676416 | bytes 8388608 | tf_op jit(solution)/shard_map/dot_general | solution.py:25
  643.4 40.4 %all-reduce = (f32[1024]{0:T(1024)}, f32[1024]{0:T(1024)}, f32[1024]{0:T(1024)}, f32[4096]{0:T(1024)}, f32[1024]{0:T(1024)}, /*index=5*/f32[1024]{0:T(1024)}, f32[1024]{0:T(1024)}) all-reduce(f32[1024]{0:T(1024)S(1)} %reshape.235, f32[1024]{0:T(1024)S(1)} %add.370, ...), channel_id=1, replica_groups=mesh['dp'=8,'seq'=4] {'dp','seq'}, use_global_device_ids=true, to_apply=%region_25.26 | all-reduce | flops 10240 | bytes 81920 | tf_op jit(solution)/shard_map/psum | solution.py:56
  (223 shorter events, 128.7 us)
Async XLA Ops:
  7.2 121.8 %copy-start.35 = (bf16[2,128,1024]{2,1,0:T(8,128)(2,1)S(1)}, bf16[2,128,1024]{2,1,0:T(8,128)(2,1)}, u32[]{:S(2)}) copy-start(bf16[2,128,1024]{2,1,0:T(8,128)(2,1)} %param.22) | copy-start | bytes 1572868
  7.2 63.2 %all-gather.9.cloned.1.call-start = ((), (), s32[]{:S(2)}) async-start(), calls=%async_computation.2 | async-start | bytes 2162688 | tf_op jit(solution)/shard_map/all_gather | solution.py:254
  8.9 120.1 %all-gather.13.cloned.1.call-start = ((), (), s32[]{:S(2)}) async-start(), calls=%async_computation.4 | async-start | bytes 2162688 | tf_op jit(solution)/shard_map/all_gather | solution.py:253
  10.5 177.1 %all-gather.11.cloned.1.call-start = ((), (), s32[]{:S(2)}) async-start(), calls=%async_computation.3 | async-start | bytes 2162688 | tf_op jit(solution)/shard_map/all_gather | solution.py:252
  12.1 233.3 %all-gather.15.cloned.1.call-start = ((), (), s32[]{:S(2)}) async-start(), calls=%async_computation.5 | async-start | bytes 2162688 | tf_op jit(solution)/shard_map/all_gather | solution.py:255
  13.7 255.1 %all-gather.21.cloned.1.call-start = ((), (), s32[]{:S(2)}) async-start(), calls=%async_computation.8 | async-start | bytes 2621440 | tf_op jit(solution)/shard_map/all_gather | solution.py:51
  73.6 58.6 %copy-start.37 = (f32[32,4096]{1,0:T(8,128)S(1)}, f32[32,4096]{1,0:T(8,128)}, u32[]{:S(2)}) copy-start(f32[32,4096]{1,0:T(8,128)} %param.31) | copy-start | bytes 1572868
  73.6 59.4 %copy-start.38 = (f32[128,1024]{1,0:T(8,128)S(1)}, f32[128,1024]{1,0:T(8,128)}, u32[]{:S(2)}) copy-start(f32[128,1024]{1,0:T(8,128)} %param.32) | copy-start | bytes 1572868
  73.6 60.2 %copy-start.54 = (s32[6]{0:T(128)S(1)}, s32[6]{0:T(128)}, u32[]{:S(2)}) copy-start(s32[6]{0:T(128)} %param.25) | copy-start | bytes 76
  73.7 60.3 %copy-start.48 = (s32[2]{0:T(128)S(1)}, s32[2]{0:T(128)}, u32[]{:S(2)}) copy-start(s32[2]{0:T(128)} %param.26) | copy-start | bytes 28
  73.7 113.9 %copy-start.51 = (f32[1024]{0:T(1024)S(1)}, f32[1024]{0:T(1024)}, u32[]{:S(2)}) copy-start(f32[1024]{0:T(1024)} %param.33) | copy-start | bytes 12292
  73.7 219.2 %all-gather.23.cloned.1.call-start = ((), (), s32[]{:S(2)}) async-start(), calls=%async_computation.9 | async-start | bytes 2621440 | tf_op jit(solution)/shard_map/all_gather | solution.py:50
  132.1 240.7 %all-gather.17.cloned.1.call-start = ((), (), s32[]{:S(2)}) async-start(), calls=%async_computation.6 | async-start | bytes 8650752 | tf_op jit(solution)/shard_map/all_gather | solution.py:256
  132.9 57.9 %copy-start.23 = (bf16[6,128,1024]{2,1,0:T(8,128)(2,1)S(1)}, bf16[6,128,1024]{2,1,0:T(8,128)(2,1)}, u32[]{:S(2)}) copy-start(bf16[6,128,1024]{2,1,0:T(8,128)(2,1)} %param.21) | copy-start | bytes 4718596
  132.9 57.9 %copy-start.50 = (f32[1024]{0:T(1024)S(1)}, f32[1024]{0:T(1024)}, u32[]{:S(2)}) copy-start(f32[1024]{0:T(1024)} %param.34) | copy-start | bytes 12292
  133.0 318.4 %all-gather.19.cloned.1.call-start = ((), (), s32[]{:S(2)}) async-start(), calls=%async_computation.7 | async-start | bytes 8650752 | tf_op jit(solution)/shard_map/all_gather | solution.py:257
  133.8 508.4 %reduce-scatter.5.cloned.1.call-start = ((), (), s32[]{:S(2)}) async-start(), calls=%async_computation.11 | async-start | bytes 2621440 | tf_op jit(solution)/shard_map/reduce_scatter | solution.py:70
  310.8 62.0 %copy-start.46 = (f32[1024]{0:T(1024)S(1)}, f32[1024]{0:T(1024)}, u32[]{:S(2)}) copy-start(f32[1024]{0:T(1024)} %param.38) | copy-start | bytes 12292
  310.8 62.0 %copy-start.49 = (f32[4096]{0:T(1024)S(1)}, f32[4096]{0:T(1024)}, u32[]{:S(2)}) copy-start(f32[4096]{0:T(1024)} %param.36) | copy-start | bytes 49156
  310.8 62.0 %copy-start.53 = (f32[1024]{0:T(1024)S(1)}, f32[1024]{0:T(1024)}, u32[]{:S(2)}) copy-start(f32[1024]{0:T(1024)} %param.39) | copy-start | bytes 12292
  312.9 138.5 %copy-start.52 = (f32[1024]{0:T(1024)S(1)}, f32[1024]{0:T(1024)}, u32[]{:S(2)}) copy-start(f32[1024]{0:T(1024)} %param.37) | copy-start | bytes 12292
  380.9 78.3 %copy-start.40 = (f32[1024]{0:T(1024)S(1)}, f32[1024]{0:T(1024)}, u32[]{:S(2)}) copy-start(f32[1024]{0:T(1024)} %param.40) | copy-start | bytes 12292
  493.2 190.5 %reduce-scatter.3.cloned.1.call-start = ((), (), s32[]{:S(2)}) async-start(), calls=%async_computation.10 | async-start | bytes 2621440 | tf_op jit(solution)/shard_map/reduce_scatter | solution.py:67
  527.0 36.4 %copy-start = (bf16[2,16,128,512]{3,2,1,0:T(8,128)(2,1)}, bf16[2,16,128,512]{3,2,1,0:T(8,128)(2,1)S(1)}, u32[]{:S(2)}) copy-start(bf16[2,16,128,512]{3,2,1,0:T(8,128)(2,1)S(1)} %multiply_convert_fusion.1) | copy-start | bytes 12582916
  (47 other events, 296.8 us)
Sparse Core Ops, SparseCore 0:
  11.4 58.9 all-gather.8
  73.9 55.0 all-gather.12
  132.4 55.0 all-gather.10
  190.3 55.0 all-gather.14
  247.4 21.4 all-gather.20
  270.2 22.5 all-gather.22
  295.7 77.0 all-gather.16
  375.7 75.6 all-gather.18
  493.3 29.7 reduce-scatter.4
  597.0 29.7 reduce-scatter.2
where the time goes:
time: 704 us; the launch traced here: 695 us
  waiting for transfers between devices  360 us (51%)
  matrix products  211 us (30%)
  blocking collectives  40.4 us (6%)
  local copies, waits for them, and re-layouts  34.1 us (5%)
  other arithmetic  33 us (5%)
  between operations  15.4 us (2%)
    all_gather x1, waiting for transfers between devices, on_device(): lax.all_gather(downward_low, ('dp', 'seq'), axis=0, tiled=True)  70.5 us
    dot_general x12, matrix products, forward_product(): return jnp.dot(left, right, preferred_element_type=jnp.float32)  70.3 us
    all_gather x1, waiting for transfers between devices, on_device(): lax.all_gather(upward_low, ('dp', 'seq'), axis=0, tiled=True)  59.9 us
    all_gather x1, waiting for transfers between devices, on_device(): lax.all_gather(value_low, ('dp', 'seq'), axis=0, tiled=True)  56.7 us
    dot_general x8, matrix products, backward_product(): lax.dot_general(left, right, (((left.ndim - 1,), (1,)), ((), ())), prefer...  55.5 us
    all_gather x1, waiting for transfers between devices, on_device(): lax.all_gather(key_low, ('dp', 'seq'), axis=0, tiled=True)  55.3 us
    all_gather x1, waiting for transfers between devices, on_device(): lax.all_gather(query_low, ('dp', 'seq'), axis=0, tiled=True)  53.6 us
    psum x1, blocking collectives, settle_each(): return lax.psum(value, ('dp', 'seq'))  40.4 us
  transfers between devices with their start and end apart: 10, of which 8 were waited for; matrix products, arithmetic and copies ran while one was open for 32% of the time, Pallas kernels for 0%

commit v1 on v0

--- a/solution.py
+++ b/solution.py
@@ -1,6 +1,10 @@
+import functools
+
 import jax
 import jax.numpy as jnp
 from jax import lax
+from jax.experimental import pallas as pl
+from jax.experimental.pallas import tpu as pltpu
 from jax.sharding import PartitionSpec as P
 
 HEADS = 16
@@ -205,6 +209,158 @@
     return (input_grad.astype(jnp.bfloat16), deltas)
 
 
+MESH = pl.DeviceIdType.MESH
+
+
+def gather_kernel(depth, wide_ref, tall_ref, wide_out, tall_out, wide_buf, tall_buf, send_sem, recv_sem, own_sem, out_sem):
+    dp = lax.axis_index("dp")
+    seq = lax.axis_index("seq")
+    z, x = dp // 2, dp % 2
+    y, c = seq // 2, seq % 2
+    x_peer = (z * 2 + (1 - x), seq)
+    y_peer = (dp, (1 - y) * 2 + c)
+    core_peer = (dp, y * 2 + (1 - c))
+    z_peers = [(lax.rem(z + k, depth) * 2 + x, seq) for k in range(1, depth)]
+    half = depth // 2
+    wide_units = wide_ref.shape[0]
+    units = wide_units + tall_ref.shape[0]
+    hops = depth - 1
+
+    own = []
+    for u in range(units):
+        src = wide_ref.at[u] if u < wide_units else tall_ref.at[u - wide_units]
+        buf = wide_buf.at[u] if u < wide_units else tall_buf.at[u - wide_units]
+        cp = pltpu.make_async_copy(src, buf.at[z, x, y, c], own_sem.at[u])
+        cp.start()
+        own.append(cp)
+
+    barrier = pltpu.get_barrier_semaphore()
+    peers = z_peers + [x_peer, y_peer, core_peer]
+    for peer in peers:
+        pl.semaphore_signal(barrier, inc=1, device_id=peer, device_id_type=MESH)
+    pl.semaphore_wait(barrier, len(peers))
+
+    def unit(u):
+        if u < wide_units:
+            return wide_ref.at[u], wide_buf.at[u], wide_out.at[u]
+        return tall_ref.at[u - wide_units], tall_buf.at[u - wide_units], tall_out.at[u - wide_units]
+
+    def remote(u, slot, src, dst, peer):
+        return pltpu.make_async_remote_copy(
+            src_ref=src, dst_ref=dst, send_sem=send_sem.at[u, slot], recv_sem=recv_sem.at[u, slot],
+            device_id=peer, device_id_type=MESH)
+
+    sends = {}
+
+    def send(u, slot, part, peer):
+        _, buf, _ = unit(u)
+        cp = remote(u, slot, buf.at[part], buf.at[part], peer)
+        cp.start()
+        sends[u, slot] = cp
+
+    lo, hi, every = pl.ds(0, half), pl.ds(half, depth - half), pl.ds(0, depth)
+    both = pl.ds(0, 2)
+    B0, B1, C0, C1, D0 = hops, hops + 1, hops + 2, hops + 3, hops + 4
+    for u in range(units):
+        src, buf, _ = unit(u)
+        for k in range(hops):
+            cp = remote(u, k, src, buf.at[z, x, y, c], z_peers[k])
+            cp.start()
+            sends[u, k] = cp
+
+    def step_a(u):
+        for k in range(hops):
+            sends[u, k].wait_recv()
+        own[u].wait()
+        send(u, B0, (lo, x, y, c), x_peer)
+        send(u, B1, (hi, x, y, c), y_peer)
+        send(u, D0, (every, x, y, c), core_peer)
+
+    def step_b(u):
+        sends[u, B0].wait_recv()
+        send(u, C0, (lo, both, y, c), y_peer)
+        sends[u, B1].wait_recv()
+        send(u, C1, (hi, x, both, c), x_peer)
+        send(u, D0 + 1, (lo, 1 - x, y, c), core_peer)
+        send(u, D0 + 2, (hi, x, 1 - y, c), core_peer)
+
+    def step_c(u):
+        sends[u, C0].wait_recv()
+        send(u, D0 + 3, (lo, both, 1 - y, c), core_peer)
+        sends[u, C1].wait_recv()
+        send(u, D0 + 4, (hi, 1 - x, both, c), core_peer)
+
+    def step_d(u):
+        for k in range(5):
+            sends[u, D0 + k].wait_recv()
+        _, buf, out = unit(u)
+        pltpu.make_async_copy(buf, out, out_sem.at[u]).start()
+
+    for i in range(units + 3):
+        if i < units:
+            step_a(i)
+        if 0 <= i - 1 < units:
+            step_b(i - 1)
+        if 0 <= i - 2 < units:
+            step_c(i - 2)
+        if 0 <= i - 3 < units:
+            step_d(i - 3)
+    for u in range(units):
+        _, buf, out = unit(u)
+        pltpu.make_async_copy(buf, out, out_sem.at[u]).wait()
+        for slot in range(hops + 9):
+            sends[u, slot].wait_send()
+
+
+def gather_weights(wide, tall):
+    dp = lax.axis_size("dp")
+    depth = dp // 2
+    lead = (depth, 2, 2, 2)
+    wide_shape = (wide.shape[0], *lead, *wide.shape[1:])
+    tall_shape = (tall.shape[0], *lead, *tall.shape[1:])
+    units = wide.shape[0] + tall.shape[0]
+    slots = depth + 8
+    anywhere = pl.BlockSpec(memory_space=pl.ANY)
+    return pl.pallas_call(
+        functools.partial(gather_kernel, depth),
+        out_shape=(jax.ShapeDtypeStruct(wide_shape, wide.dtype), jax.ShapeDtypeStruct(tall_shape, tall.dtype)),
+        in_specs=[anywhere] * 2,
+        out_specs=(anywhere,) * 2,
+        scratch_shapes=[
+            pltpu.VMEM(wide_shape, wide.dtype),
+            pltpu.VMEM(tall_shape, tall.dtype),
+            pltpu.SemaphoreType.DMA((units, slots)),
+            pltpu.SemaphoreType.DMA((units, slots)),
+            pltpu.SemaphoreType.DMA((units,)),
+            pltpu.SemaphoreType.DMA((units,)),
+        ],
+        compiler_params=pltpu.CompilerParams(
+            collective_id=0, has_side_effects=True, vmem_limit_bytes=60 * 2**20),
+        name="gather_weights",
+    )(wide, tall)
+
+
+def gather_all(lows):
+    query_low, key_low, value_low, output_low, upward_low, downward_low = lows
+    rows, width = query_low.shape
+    devices = lax.axis_size("dp") * lax.axis_size("seq")
+    if rows % 16 or lax.axis_size("seq") != 4 or lax.axis_size("dp") % 4:
+        return tuple(lax.all_gather(low, ("dp", "seq"), axis=0, tiled=True) for low in lows)
+    strips = upward_low.shape[1] // width
+    slim = width // 4
+    wide = jnp.stack(
+        [query_low, key_low, value_low, output_low]
+        + [upward_low[:, i * width : (i + 1) * width] for i in range(strips)]
+    )
+    tall = jnp.stack([downward_low[:, i * slim : (i + 1) * slim] for i in range(4)])
+    wide_all, tall_all = gather_weights(wide, tall)
+    wide_all = wide_all.reshape(wide.shape[0], devices * rows, width)
+    tall_all = tall_all.reshape(4, devices * downward_low.shape[0], slim)
+    upward_all = jnp.concatenate([wide_all[4 + i] for i in range(strips)], axis=1)
+    downward_all = jnp.concatenate([tall_all[i] for i in range(4)], axis=1)
+    return (wide_all[0], wide_all[1], wide_all[2], wide_all[3], upward_all, downward_all)
+
+
 def on_device(
     short_input,
     long_input,
@@ -248,24 +404,11 @@
     output_low = output_weight.astype(jnp.bfloat16)
     upward_low = upward_weight.astype(jnp.bfloat16)
     downward_low = downward_weight.astype(jnp.bfloat16)
-    gathered = (
-        lax.all_gather(query_low, ("dp", "seq"), axis=0, tiled=True),
-        lax.all_gather(key_low, ("dp", "seq"), axis=0, tiled=True),
-        lax.all_gather(value_low, ("dp", "seq"), axis=0, tiled=True),
-        lax.all_gather(output_low, ("dp", "seq"), axis=0, tiled=True),
-        lax.all_gather(upward_low, ("dp", "seq"), axis=0, tiled=True),
-        lax.all_gather(downward_low, ("dp", "seq"), axis=0, tiled=True),
-    )
+    lows = (query_low, key_low, value_low, output_low, upward_low, downward_low)
+    gathered = gather_all(lows)
     short_output = recompute(short_input, short_usable, gathered, params, keep_local)[-1]
     long_output = recompute(long_input, long_usable, gathered, params, spread_long)[-1]
-    regathered = (
-        lax.all_gather(query_low, ("dp", "seq"), axis=0, tiled=True),
-        lax.all_gather(key_low, ("dp", "seq"), axis=0, tiled=True),
-        lax.all_gather(value_low, ("dp", "seq"), axis=0, tiled=True),
-        lax.all_gather(output_low, ("dp", "seq"), axis=0, tiled=True),
-        lax.all_gather(upward_low, ("dp", "seq"), axis=0, tiled=True),
-        lax.all_gather(downward_low, ("dp", "seq"), axis=0, tiled=True),
-    )
+    regathered = gathered
     short_grad, short_deltas = backprop(
         short_input,
         short_cotangent,

time: 704 us -> 443 us (0.63)
  waiting for transfers between devices: 360 us -> 0.09 us
  Pallas kernels: 0 us -> 124 us
  matrix products: 211 us -> 194 us
  other arithmetic: 33 us -> 23 us
    all_gather x6 -> x0, waiting for transfers between devices: 322 us -> none  [the longest x1 70.5 us: on_device(): lax.all_gather(downward_low, ('dp', 'seq'), axis=0, tiled=True)]
    pallas_call x0 -> x1, Pallas kernels: none -> 124 us  [gather_weights(): pl.pallas_call(functools.partial(gather_kernel, depth), out_shape=(jax.Sh...]
    all_gather x1, waiting for transfers between devices: 20 us -> 0.02 us  [spread_long(): lax.all_gather(key_rows, 'seq', axis=1, tiled=True)]
    all_gather x1, waiting for transfers between devices: 17.8 us -> 0.01 us  [spread_long(): lax.all_gather(values, 'seq', axis=1, tiled=True)]
    slice x0 -> x2, local copies, waits for them, and re-layouts: none -> 16 us  [the longest x1 11.7 us: gather_all(): wide_all[4 + i]]
    dot_general x12, matrix products: 70.3 us -> 55.6 us  [forward_product(): return jnp.dot(left, right, preferred_element_type=jnp.float32)]
    all_gather x2 -> x0, local copies, waits for them, and re-layouts: 8.18 us -> none  [the longest x1 4.21 us: spread_long(): lax.all_gather(key_rows, 'seq', axis=1, tiled=True)]
    convert_element_type x2, other arithmetic: 11.2 us -> 3.45 us  [backprop(): score_grad = score_grad.astype(jnp.bfloat16)]
  transfers between devices with their start and end apart: 10 -> 4, of which waited for: 8 -> 0; matrix products, arithmetic and copies ran while one was open for 32% -> 40% of each run, Pallas kernels for 0% -> 0%
where the time goes in v1:
time: 443 us; the launch traced here: 438 us
  matrix products  194 us (44%)
  Pallas kernels  124 us (28%)
  blocking collectives  45 us (10%)
  local copies, waits for them, and re-layouts  36.6 us (8%)
  other arithmetic  23 us (5%)
  between operations  15 us (3%)
    pallas_call x1, Pallas kernels, gather_weights(): pl.pallas_call(functools.partial(gather_kernel, depth), out_shape=(jax.Sh...  124 us
    dot_general x8, matrix products, backward_product(): lax.dot_general(left, right, (((left.ndim - 1,), (1,)), ((), ())), prefer...  57.3 us
    dot_general x12, matrix products, forward_product(): return jnp.dot(left, right, preferred_element_type=jnp.float32)  55.6 us
    psum x1, blocking collectives, settle_each(): return lax.psum(value, ('dp', 'seq'))  45 us
    dot_general x4, matrix products, exact_backward(): lax.dot_general(left, right, (((left.ndim - 1,), (1,)), ((), ())), precis...  25.8 us
    dot_general x2, matrix products, backprop(): jnp.einsum('nhqk,nqhd->nkhd', attention_low, blended_grad, preferred_elem...  12.7 us
    sub x2, matrix products, recompute(): attention = jax.nn.softmax(scores, axis=-1)  12.3 us
    slice x1, local copies, waits for them, and re-layouts, gather_all(): wide_all[4 + i]  11.7 us
  transfers between devices with their start and end apart: 4, of which 0 were waited for; matrix products, arithmetic and copies ran while one was open for 40% of the time, Pallas kernels for 0%

profile of v1, /device:TPU:0, one launch (start us, length us, event | category | flops | bytes accessed | tf_op | source)
XLA Modules:
  0.0 438.4 jit_solution(12858094244701509618)
XLA Ops:
  14.0 123.7 %gather_weights.1 = (bf16[8,4,2,2,2,32,1024]{6,5,4,3,2,1,0:T(8,128)(2,1)}, bf16[4,4,2,2,2,128,256]{6,5,4,3,2,1,0:T(8,128)(2,1)}) custom-call(bf16[8,32,1024]{2,1,0:T(8,128)(2,1)} %copy-done.47, bf16[4,128,256]{2,1,0:T(8,128)(2,1)} %pad_maximum_fusion.tall_ref), custom_call_target="tpu_custom_call" | custom-call | tf_op jit(solution)/shard_map/gather_weights/pallas_call | solution.py:324
  137.7 11.7 %fusion.113 = (bf16[1,4,2,2,2,32,1024]{6,5,4,3,2,1,0:T(8,128)(2,1)}, bf16[1,4,2,2,2,32,1024]{6,5,4,3,2,1,0:T(8,128)(2,1)}, bf16[1,4,2,2,2,32,1024]{6,5,4,3,2,1,0...) fusion(bf16[8,4,2,2,2,32,1024]{6,5,4,3,2,1,0:T(8,128)(2,1)} %ge, ...), kind=kLoop, calls=%fused_computation.200 | loop fusion | bytes 33554432 | tf_op jit(solution)/shard_map/slice | solution.py:359
  154.9 4.6 %convolution_convert_fusion.2 = bf16[1024,6,128]{2,0,1:T(8,128)(2,1)} fusion(bf16[1024,1024,1]{1,0,2:T(8,128)(2,1)S(1)} %bitcast.194, bf16[6,128,1024]{2,1,0:T(8,128)(2,1)} %param.21), kind=kOutput, calls=%fused_computation.86 | convolution fusion | flops 1611399168 | bytes 5242880 | tf_op jit(solution)/shard_map/dot_general | solution.py:19
  165.2 4.5 %fusion.116 = (f32[6,16,128]{2,1,0:T(8,128)S(1)}, f32[6,16,128,128]{2,3,1,0:T(8,128)}) fusion(pred[6,128]{1,0:T(8,128)(4,1)S(1)} %iota_compare_fusion.1, bf16[6,128,16,64]{1,3,2,0:T(8,128)(2,1)S(1)} %bitcast.253, bf16[6,128,16,64]{1,3,2,0:T(8,128)(2,1)S(1)} %bitcast.249), kind=kOutput, calls=%fused_computation.203 | convolution fusion | flops 207618176 | bytes 9487104 | tf_op jit(solution)/shard_map/sub | solution.py:108
  169.7 4.5 %convolution_convert_fusion.1 = bf16[6,16,64,128]{3,2,1,0:T(8,128)(2,1)S(1)} fusion(bf16[6,128,16,64]{1,3,2,0:T(8,128)(2,1)} %bitcast.263, f32[6,16,128,128]{2,3,1,0:T(8,128)} %get-tuple-element.63, f32[6,16,128]{2,1,0:T(8,128)S(1)} %get-tuple-element.62), kind=kOutput, calls=%fused_computation.85 | convolution fusion | flops 205258752 | bytes 9486336 | tf_op jit(solution)/shard_map/nhqk,nkhd->nqhd/dot_general | solution.py:110
  176.8 4.3 fusion.114
  182.6 13.0 %fusion.45 = f32[6,128,4096]{2,1,0:T(8,128)} fusion(f32[6,128,1024]{2,1,0:T(8,128)S(1)} %get-tuple-element.65, f32[1024]{0:T(1024)S(1)} %copy-done.64, f32[1024]{0:T(1024)S(1)} %copy-done.55, f32[6,128]{1,0:T(8,128)S(1)} %fusion.91, f32[6,128]{1,0:T(8,128)S(1)} %broadcast_multiply_fusion.1, bf16[1024,1024]{1,0:T(8,128)(2,1)S(1)} %bitcast.217, ...), kind=kOutput, calls=%fused_computation.87 | convolution fusion | flops 6479937536 | bytes 24131584 | tf_op jit(solution)/shard_map/dot_general | solution.py:19
  195.6 12.7 %fusion.118 = (f32[6,128]{1,0:T(8,128)S(1)}, f32[6,128,1024]{2,1,0:T(8,128)S(1)}) fusion(f32[1024]{0:T(1024)S(1)} %copy-done.63, bf16[4096,256]{1,0:T(8,128)(2,1)} %bitcast.236, bf16[4096,256]{1,0:T(8,128)(2,1)} %bitcast.240, bf16[4096,256]{1,0:T(8,128)(2,1)} %bitcast.244, bf16[4096,256]{1,0:T(8,128)(2,1)} %bitcast.232, f32[6,128,4096]{2,1,0:T(8,128)} %fusion.45, ...), kind=kOutput, calls=%fused_computation.205 | convolution fusion | flops 6512966656 | bytes 27300864 | tf_op jit(solution)/shard_map/dot_general | solution.py:19
  210.3 22.7 %fusion.122 = (f32[4096]{0:T(1024)}, bf16[6,128,4096]{2,1,0:T(8,128)(2,1)}) fusion(f32[6,128,4096]{2,1,0:T(8,128)} %fusion.45, f32[4096]{0:T(1024)S(1)} %copy-done.60, bf16[4096,256]{1,0:T(8,128)(2,1)} %bitcast.237, bf16[4096,256]{1,0:T(8,128)(2,1)} %bitcast.241, bf16[4096,256]{1,0:T(8,128)(2,1)} %bitcast.245, bf16[4096,256]{1,0:T(8,128)(2,1)} %bitcast.233, ...), kind=kOutput, calls=%fused_computation.209 | convolution fusion | flops 6552285184 | bytes 32030720 | tf_op jit(solution)/shard_map/dot_general | solution.py:23
  233.0 12.4 %fusion.109 = (f32[1024]{0:T(1024)S(1)}, f32[6,128]{1,0:T(8,128)S(1)}, f32[6,128,1024]{2,1,0:T(8,128)S(1)}) fusion(f32[1024]{0:T(1024)S(1)} %copy-done.55, f32[6,128,1024]{2,1,0:T(8,128)S(1)} %get-tuple-element.65, f32[6,128]{1,0:T(8,128)S(1)} %broadcast_multiply_fusion.1, bf16[1024,1024]{1,0:T(8,128)(2,1)} %bitcast.216, bf16[1024,1024]{1,0:T(8,128)(2,1)} %bitcast.220, ...), kind=kOutput, calls=%fused_computation.196 | convolution fusion | flops 6487013376 | bytes 25720832 | tf_op jit(solution)/shard_map/dot_general | solution.py:23
  256.3 4.5 %multiply_reduce_fusion.1 = (f32[6,16,128]{2,1,0:T(8,128)S(1)}, f32[6,16,128,128]{2,3,1,0:T(8,128)S(1)}) fusion(f32[6,16,128,128]{2,3,1,0:T(8,128)} %get-tuple-element.63, f32[6,16,128]{2,1,0:T(8,128)S(1)} %get-tuple-element.62, bf16[6,128,16,64]{1,3,2,0:T(8,128)(2,1)S(1)} %bitcast.251, bf16[6,128,16,64]{1,3,2,0:T(8,128)(2,1)S(1)} %bitcast.264), kind=kOutput, calls=%fused_computation.19 | convolution fusion | flops 206032896 | bytes 15826944 | tf_op jit(solution)/shard_map/nqhd,nkhd->nhqk/dot_general | solution.py:176
  262.9 7.8 %fusion.119 = (f32[2,16,128]{2,1,0:T(8,128)S(1)}, f32[2,16,128,512]{3,2,1,0:T(8,128)}) fusion(pred[2,512]{1,0:T(4,128)(4,1)S(1)} %iota_compare_fusion, bf16[2,128,16,64]{1,3,2,0:T(8,128)(2,1)} %bitcast.258, bf16[2,512,16,64]{1,3,2,0:T(8,128)(2,1)} %bitcast.229), kind=kOutput, calls=%fused_computation.206 | convolution fusion | flops 276824576 | bytes 11027456 | tf_op jit(solution)/shard_map/sub | solution.py:108
  270.7 5.8 %fusion.65 = bf16[2,16,64,128]{3,2,1,0:T(8,128)(2,1)S(1)} fusion(bf16[2,512,16,64]{1,3,2,0:T(8,128)(2,1)} %bitcast.260, f32[2,16,128,512]{3,2,1,0:T(8,128)} %get-tuple-element.69, f32[2,16,128]{2,1,0:T(8,128)S(1)} %get-tuple-element.68), kind=kOutput, calls=%fused_computation.114 | convolution fusion | flops 272891904 | bytes 11026432 | tf_op jit(solution)/shard_map/nhqk,nkhd->nqhd/dot_general | solution.py:110
  278.8 4.5 %convolution_add_fusion = f32[2,128,4096]{2,1,0:T(8,128)} fusion(f32[4096]{0:T(1024)S(1)} %copy-done.60, f32[2,128,1024]{2,1,0:T(8,128)S(1)} %get-tuple-element.71, f32[1024]{0:T(1024)S(1)} %copy-done.64, f32[1024]{0:T(1024)S(1)} %copy-done.55, f32[2,128]{1,0:T(2,128)S(1)} %fusion.93, f32[2,128]{1,0:T(2,128)S(1)} %broadcast_multiply_fusion.3, ...), kind=kOutput, calls=%fused_computation.27 | convolution fusion | flops 2183397376 | bytes 13658112 | tf_op jit(solution)/shard_map/dot_general | solution.py:19
  283.3 6.1 %fusion.121 = (f32[2,128]{1,0:T(2,128)S(1)}, f32[2,128,1024]{2,1,0:T(8,128)S(1)}) fusion(f32[1024]{0:T(1024)S(1)} %copy-done.63, bf16[4096,256]{1,0:T(8,128)(2,1)} %bitcast.238, bf16[4096,256]{1,0:T(8,128)(2,1)} %bitcast.242, bf16[4096,256]{1,0:T(8,128)(2,1)} %bitcast.246, bf16[4096,256]{1,0:T(8,128)(2,1)S(1)} %bitcast.235, ...), kind=kOutput, calls=%fused_computation.208 | convolution fusion | flops 2192310016 | bytes 14695424 | tf_op jit(solution)/shard_map/dot_general | solution.py:19
  290.2 9.0 %fusion.123 = (f32[4096]{0:T(1024)S(1)}, bf16[2,128,4096]{2,1,0:T(8,128)(2,1)}) fusion(f32[2,128,4096]{2,1,0:T(8,128)} %convolution_add_fusion, bf16[4096,256]{1,0:T(8,128)(2,1)} %bitcast.239, bf16[4096,256]{1,0:T(8,128)(2,1)} %bitcast.243, bf16[4096,256]{1,0:T(8,128)(2,1)} %bitcast.247, bf16[4096,256]{1,0:T(8,128)(2,1)} %bitcast.234, ...), kind=kOutput, calls=%fused_computation.210 | convolution fusion | flops 2205413376 | bytes 16277504 | tf_op jit(solution)/shard_map/dot_general | solution.py:23
  299.2 5.0 %fusion.110 = (f32[1024]{0:T(1024)S(1)}, f32[2,128]{1,0:T(2,128)S(1)}, f32[2,128,1024]{2,1,0:T(8,128)S(1)}) fusion(f32[1024]{0:T(1024)S(1)} %copy-done.55, f32[2,128,1024]{2,1,0:T(8,128)S(1)} %get-tuple-element.71, f32[2,128]{1,0:T(2,128)S(1)} %broadcast_multiply_fusion.3, bf16[1024,1024]{1,0:T(8,128)(2,1)S(1)} %bitcast.219, ...), kind=kOutput, calls=%fused_computation.197 | convolution fusion | flops 2184706816 | bytes 14174208 | tf_op jit(solution)/shard_map/dot_general | solution.py:23
  309.2 5.7 %fusion.40 = bf16[2,16,64,512]{3,2,1,0:T(8,128)(2,1)} fusion(bf16[2,128,16,64]{1,3,2,0:T(8,128)(2,1)} %bitcast.256, f32[2,16,128,512]{3,2,1,0:T(8,128)} %get-tuple-element.69, f32[2,16,128]{2,1,0:T(8,128)S(1)} %get-tuple-element.68), kind=kOutput, calls=%fused_computation.82 | convolution fusion | flops 273678336 | bytes 11026432 | tf_op jit(solution)/shard_map/nhqk,nqhd->nkhd/dot_general | solution.py:189
  319.2 4.7 %bitcast_convert_fusion = (bf16[6,128,16,64]{1,3,2,0:T(8,128)(2,1)}, f32[6,16,64,128]{3,2,1,0:T(8,128)}) fusion(bf16[6,128,16,64]{1,3,2,0:T(8,128)(2,1)} %bitcast.248, bf16[6,16,128,128]{2,3,1,0:T(8,128)(2,1)S(1)} %multiply_convert_fusion.2), kind=kOutput, calls=%fused_computation.50 | convolution fusion | flops 202899456 | bytes 9437184 | tf_op jit(solution)/shard_map/nhqk,nkhd->nqhd/dot_general | solution.py:181
  324.2 7.0 %bitcast_reduce_fusion = (f32[16,64]{1,0:T(8,128)S(1)}, f32[6,16,64,128]{3,2,1,0:T(8,128)}) fusion(bf16[6,128,16,64]{1,3,2,0:T(8,128)(2,1)S(1)} %bitcast.252, f32[6,16,128,128]{2,3,1,0:T(8,128)} %get-tuple-element.63, f32[6,16,128]{2,1,0:T(8,128)S(1)} %get-tuple-element.62), kind=kOutput, calls=%fused_computation.48 | convolution fusion | flops 205257728 | bytes 11063296 | tf_op jit(solution)/shard_map/nhqk,nqhd->nkhd/dot_general | solution.py:189
  338.0 4.1 copy.72
  353.5 10.1 %fusion.125 = f32[6,128,1024]{2,1,0:T(8,128)S(1)} fusion(f32[6,128,1024]{1,2,0:T(8,128)S(1)} %bitcast.210, bf16[1024,1024,1]{1,0,2:T(8,128)(2,1)S(1)} %bitcast.195), kind=kOutput, calls=%fused_computation.212 | convolution fusion | flops 9663676416 | bytes 8388608 | tf_op jit(solution)/shard_map/dot_general | solution.py:29
  363.7 12.1 %add_convert_fusion = bf16[6,128,1024]{2,1,0:T(8,128)(2,1)} fusion(f32[6,128,1024]{2,1,0:T(8,128)S(1)} %fusion.125, f32[6,128,1024]{2,1,0:T(8,128)S(1)} %fusion.124, f32[6,128,1024]{2,1,0:T(8,128)S(1)} %copy-done.11, f32[6,128,1024]{1,2,0:T(8,128)S(1)} %bitcast.262, bf16[1024,1024,1]{1,0,2:T(8,128)(2,1)S(1)} %bitcast.203, f32[6,128]{1,0:T(8,128)S(1)} %negate_multiply_fusion), kind=kOutput, calls=%fused_computation.51 | convolution fusion | flops 9667608576 | bytes 16256000 | tf_op jit(solution)/shard_map/dot_general | solution.py:29
  383.1 45.0 %all-reduce = (f32[1024]{0:T(1024)}, f32[1024]{0:T(1024)}, f32[1024]{0:T(1024)}, f32[4096]{0:T(1024)}, f32[1024]{0:T(1024)}, /*index=5*/f32[1024]{0:T(1024)}, f32[1024]{0:T(1024)}) all-reduce(f32[1024]{0:T(1024)S(1)} %reshape.256, f32[1024]{0:T(1024)S(1)} %add.374, ...), channel_id=1, replica_groups=mesh['dp'=8,'seq'=4] {'dp','seq'}, use_global_device_ids=true, to_apply=%region_25.26 | all-reduce | flops 10240 | bytes 81920 | tf_op jit(solution)/shard_map/psum | solution.py:60
  (236 shorter events, 77.9 us)
Async XLA Ops:
  7.2 255.7 %all-gather.5.cloned.1.call-start = ((), (), s32[]{:S(2)}) async-start(), calls=%async_computation.3 | async-start | bytes 2621440 | tf_op jit(solution)/shard_map/all_gather | solution.py:54
  137.6 11.8 %copy-start.48 = (bf16[2,128,1024]{2,1,0:T(8,128)(2,1)S(1)}, bf16[2,128,1024]{2,1,0:T(8,128)(2,1)}, u32[]{:S(2)}) copy-start(bf16[2,128,1024]{2,1,0:T(8,128)(2,1)} %param.22) | copy-start | bytes 1572868
  151.0 119.6 %all-gather.3.cloned.1.call-start = ((), (), s32[]{:S(2)}) async-start(), calls=%async_computation.2 | async-start | bytes 2621440 | tf_op jit(solution)/shard_map/all_gather | solution.py:55
  154.3 227.6 %reduce-scatter.5.cloned.1.call-start = ((), (), s32[]{:S(2)}) async-start(), calls=%async_computation.5 | async-start | bytes 2621440 | tf_op jit(solution)/shard_map/reduce_scatter | solution.py:74
  169.7 7.1 %slice-start.2 = ((s8[8388608]{0:T(1024)(128)(4,1)}), s8[4194304]{0:T(1024)(128)(4,1)S(1)}, s32[]{:S(2)}) async-start(s8[8388608]{0:T(1024)(128)(4,1)} %bitcast.205), calls=%async_computation.8 | async-start | bytes 8388608
  169.7 7.1 %slice-start.3 = ((s8[8388608]{0:T(1024)(128)(4,1)}), s8[4194304]{0:T(1024)(128)(4,1)S(1)}, s32[]{:S(2)}) async-start(s8[8388608]{0:T(1024)(128)(4,1)} %bitcast.205), calls=%async_computation.9 | async-start | bytes 8388608
  182.6 13.0 %copy-start.60 = (f32[4096]{0:T(1024)S(1)}, f32[4096]{0:T(1024)}, u32[]{:S(2)}) copy-start(f32[4096]{0:T(1024)} %param.36) | copy-start | bytes 49156
  182.6 13.0 %copy-start.63 = (f32[1024]{0:T(1024)S(1)}, f32[1024]{0:T(1024)}, u32[]{:S(2)}) copy-start(f32[1024]{0:T(1024)} %param.37) | copy-start | bytes 12292
  195.6 12.8 %copy-start.7 = (bf16[6,128,1024]{2,1,0:T(8,128)(2,1)S(1)}, bf16[6,128,1024]{2,1,0:T(8,128)(2,1)}, u32[]{:S(2)}) copy-start(bf16[6,128,1024]{2,1,0:T(8,128)(2,1)} %param.23) | copy-start | bytes 4718596
  195.6 12.8 %copy-start.53 = (f32[1024]{0:T(1024)S(1)}, f32[1024]{0:T(1024)}, u32[]{:S(2)}) copy-start(f32[1024]{0:T(1024)} %param.40) | copy-start | bytes 12292
  270.7 7.0 %copy-start.37 = (bf16[1,4,2,2,2,32,1024]{6,5,4,3,2,1,0:T(8,128)(2,1)S(1)}, bf16[1,4,2,2,2,32,1024]{6,5,4,3,2,1,0:T(8,128)(2,1)}, u32[]{:S(2)}) copy-start(bf16[1,4,2,2,2,32,1024]{6,5,4,3,2,1,0:T(8,128)(2,1)} %get-tuple-element.41) | copy-start | bytes 6291460
  289.4 9.9 %copy-start.14 = (f32[2,128,1024]{2,1,0:T(8,128)}, f32[2,128,1024]{2,1,0:T(8,128)S(1)}, u32[]{:S(2)}) copy-start(f32[2,128,1024]{2,1,0:T(8,128)S(1)} %get-tuple-element.73) | copy-start | bytes 3145732
  318.9 109.2 %reduce-scatter.3.cloned.1.call-start = ((), (), s32[]{:S(2)}) async-start(), calls=%async_computation.4 | async-start | bytes 2621440 | tf_op jit(solution)/shard_map/reduce_scatter | solution.py:71
  323.9 7.3 %slice-start = ((s8[8388608]{0:T(1024)(128)(4,1)}), s8[4194304]{0:T(1024)(128)(4,1)S(1)}, s32[]{:S(2)}) async-start(s8[8388608]{0:T(1024)(128)(4,1)} %bitcast.191), calls=%async_computation.6 | async-start | bytes 8388608
  324.2 7.0 %slice-start.1 = ((s8[8388608]{0:T(1024)(128)(4,1)}), s8[4194304]{0:T(1024)(128)(4,1)S(1)}, s32[]{:S(2)}) async-start(s8[8388608]{0:T(1024)(128)(4,1)} %bitcast.191), calls=%async_computation.7 | async-start | bytes 8388608
  324.2 7.0 %copy-start.51 = (bf16[2,128,1024]{1,2,0:T(8,128)(2,1)S(1)}, bf16[2,128,1024]{1,2,0:T(8,128)(2,1)}, u32[]{:S(2)}) copy-start(bf16[2,128,1024]{1,2,0:T(8,128)(2,1)} %copy.70) | copy-start | bytes 1572868
  324.2 7.3 %copy-start.59 = (bf16[2,512,1024]{1,2,0:T(8,128)(2,1)S(1)}, bf16[2,512,1024]{1,2,0:T(8,128)(2,1)}, u32[]{:S(2)}) copy-start(bf16[2,512,1024]{1,2,0:T(8,128)(2,1)} %all-gather.3.cloned.1.call-done) | copy-start | bytes 6291460
  353.5 10.2 %copy-start.11 = (f32[6,128,1024]{2,1,0:T(8,128)S(1)}, f32[6,128,1024]{2,1,0:T(8,128)}, u32[]{:S(2)}) copy-start(f32[6,128,1024]{2,1,0:T(8,128)} %copy-done.9) | copy-start | bytes 9437188
  353.5 10.2 %copy-start.24 = (bf16[1,4,2,2,2,32,1024]{6,5,4,3,2,1,0:T(8,128)(2,1)S(1)}, bf16[1,4,2,2,2,32,1024]{6,5,4,3,2,1,0:T(8,128)(2,1)}, u32[]{:S(2)}) copy-start(bf16[1,4,2,2,2,32,1024]{6,5,4,3,2,1,0:T(8,128)(2,1)} %get-tuple-element.45) | copy-start | bytes 6291460
  353.5 10.2 %copy-start.66 = (f32[6,16,64,128]{3,2,1,0:T(8,128)S(1)}, f32[6,16,64,128]{3,2,1,0:T(8,128)}, u32[]{:S(2)}) copy-start(f32[6,16,64,128]{3,2,1,0:T(8,128)} %get-tuple-element.84) | copy-start | bytes 9437188
  363.7 12.1 %copy-start.1 = (bf16[2,16,128,512]{3,2,1,0:T(8,128)(2,1)S(1)}, bf16[2,16,128,512]{3,2,1,0:T(8,128)(2,1)}, u32[]{:S(2)}) copy-start(bf16[2,16,128,512]{3,2,1,0:T(8,128)(2,1)} %copy-done) | copy-start | bytes 12582916
  363.7 12.1 %copy-start.39 = (bf16[2,512,1024]{1,2,0:T(8,128)(2,1)S(1)}, bf16[2,512,1024]{1,2,0:T(8,128)(2,1)}, u32[]{:S(2)}) copy-start(bf16[2,512,1024]{1,2,0:T(8,128)(2,1)} %all-gather.5.cloned.1.call-done) | copy-start | bytes 6291460
  379.6 48.5 %copy-start.18 = (bf16[1,4,2,2,2,32,1024]{6,5,4,3,2,1,0:T(8,128)(2,1)S(1)}, bf16[1,4,2,2,2,32,1024]{6,5,4,3,2,1,0:T(8,128)(2,1)}, u32[]{:S(2)}) copy-start(bf16[1,4,2,2,2,32,1024]{6,5,4,3,2,1,0:T(8,128)(2,1)} %copy-done.16) | copy-start | bytes 6291460
  381.9 48.2 %copy-start.28 = (f32[2,128,1024]{2,1,0:T(8,128)S(1)}, f32[2,128,1024]{2,1,0:T(8,128)}, u32[]{:S(2)}) copy-start(f32[2,128,1024]{2,1,0:T(8,128)} %convolution_add_fusion.2) | copy-start | bytes 3145732
  (54 other events, 187.2 us)
Sparse Core Ops, SparseCore 0:
  151.2 25.3 all-gather.4
  178.7 22.8 all-gather.2
  319.1 34.0 reduce-scatter.4
  355.5 31.1 reduce-scatter.2

commit v2 on v0

v2 whole, which is shorter than its diff:
```python
import functools

import jax
import jax.numpy as jnp
from jax import lax
from jax.experimental import pallas as pl
from jax.experimental.pallas import tpu as pltpu
from jax.sharding import PartitionSpec as P

MESH = pl.DeviceIdType.MESH
F32 = jnp.float32
BF16 = jnp.bfloat16
EPSILON = 1e-12
MASKED = -1e30
SCALE = 0.125
PAIR = 128
BLOCK = 128
CHUNK = 256
TILE = 256
K_UNIT, V_UNIT, Q_UNIT, O_UNIT, UP_UNIT = 0, 1, 2, 3, 4
Q_BIAS, V_BIAS, O_BIAS, D_BIAS, GAIN1, SHIFT1, GAIN2, SHIFT2, U_BIAS = 0, 1, 2, 3, 4, 5, 6, 7, 8
Q_SUM, V_SUM, O_SUM, D_SUM, F_SUM, S_SUM, U_SUM = 0, 1, 2, 3, 4, 5, 6
SUMS = 16


def dot_nn(a, b):
    return jnp.dot(a, b, preferred_element_type=F32)


def dot_nt(a, b):
    return lax.dot_general(a, b, (((1,), (1,)), ((), ())), preferred_element_type=F32)


def dot_tn(a, b):
    return lax.dot_general(a, b, (((0,), (0,)), ((), ())), preferred_element_type=F32)


def flipped(index, bit):
    return index + bit * (1 - 2 * ((index // bit) % 2))


def gelu(u):
    return 0.5 * u * (1.0 + jnp.tanh(0.7978845608028654 * (u + 0.044715 * (u * u * u))))


def gelu_slope(u):
    square = u * u
    t = jnp.tanh(0.7978845608028654 * (u + 0.044715 * (u * square)))
    return 0.5 * (1.0 + t) + 0.5 * u * (1.0 - t * t) * (0.7978845608028654 * (1.0 + 3 * 0.044715 * square))


def step_kernel(
    remote, dp_size, seq_size, nshort,
    wsh, xs, xl, dys, dyl, short_len, long_len, par,
    so, lo, sg, lg, sums,
    w, x, q, k, v, kv_sib, dkv_in, g, r, a16, u16, f, dy, acc, acc_in,
    send_sem, recv_sem, misc_send, misc_recv, own_sem, load_sem, store_sem,
):
    dp = lax.axis_index("dp")
    seq = lax.axis_index("seq")
    y, c = seq // 2, seq % 2
    y_peer = (dp, flipped(seq, 2))
    core_peer = (dp, flipped(seq, 1))
    total, width = x.shape
    short_rows = nshort * BLOCK
    units = w.shape[0]
    depth = w.shape[1]
    hidden_chunks = (units - 4) // 2
    partners = []
    bit = 1
    while bit < seq_size:
        partners.append((dp, flipped(seq, bit)))
        bit *= 2
    bit = 1
    while bit < dp_size:
        partners.append((flipped(dp, bit), seq))
        bit *= 2

    loads = [pltpu.make_async_copy(xs, x.at[pl.ds(0, short_rows)], load_sem.at[0]),
             pltpu.make_async_copy(xl.at[y], x.at[pl.ds(short_rows + BLOCK * y, BLOCK)], load_sem.at[1])]
    late = [pltpu.make_async_copy(dys, dy.at[pl.ds(0, short_rows)], load_sem.at[2]),
            pltpu.make_async_copy(dyl.at[y], dy.at[pl.ds(short_rows + BLOCK * y, BLOCK)], load_sem.at[3])]
    for cp in loads:
        cp.start()

    if remote:
        z, ax = dp // 2, dp % 2
        hops = depth - 1
        z_peers = [((z + n) % depth * 2 + ax, seq) for n in range(1, depth)]
        x_peer = (flipped(dp, 1), seq)
        peers = z_peers + [x_peer, y_peer, core_peer]
        own = [pltpu.make_async_copy(wsh.at[u], w.at[u, z, ax, y, c], own_sem.at[u]) for u in range(units)]
    else:
        peers = partners
        own = [pltpu.make_async_copy(wsh.at[u], w.at[u], own_sem.at[u]) for u in range(units)]
    for cp in own:
        cp.start()

    barrier = pltpu.get_barrier_semaphore()
    for peer in peers:
        pl.semaphore_signal(barrier, inc=1, device_id=peer, device_id_type=MESH)
    pl.semaphore_wait(barrier, len(peers))

    def misc(slot, src, dst, peer):
        return pltpu.make_async_remote_copy(
            src_ref=src, dst_ref=dst, send_sem=misc_send.at[slot], recv_sem=misc_recv.at[slot],
            device_id=peer, device_id_type=MESH)

    swap_x = misc(0, xl.at[1 - y], x.at[pl.ds(short_rows + BLOCK * y, BLOCK)], y_peer)
    swap_dy = misc(1, dyl.at[1 - y], dy.at[pl.ds(short_rows + BLOCK * y, BLOCK)], y_peer)
    swap_x.start()

    sends = {}
    if remote:
        half = depth // 2
        lower, upper, every, both = pl.ds(0, half), pl.ds(half, depth - half), pl.ds(0, depth), pl.ds(0, 2)
        B0, B1, C0, C1, D0 = hops, hops + 1, hops + 2, hops + 3, hops + 4

        def send(u, slot, src, part, peer):
            cp = pltpu.make_async_remote_copy(
                src_ref=src, dst_ref=w.at[(u, *part)], send_sem=send_sem.at[u, slot], recv_sem=recv_sem.at[u, slot],
                device_id=peer, device_id_type=MESH)
            cp.start()
            sends[u, slot] = cp

        def pass_on(u, slot, part, peer):
            send(u, slot, w.at[(u, *part)], part, peer)

        for u in range(units):
            for n in range(hops):
                send(u, n, wsh.at[u], (z, ax, y, c), z_peers[n])

        def step_a(u):
            for n in range(hops):
                sends[u, n].wait_recv()
            own[u].wait()
            pass_on(u, B0, (lower, ax, y, c), x_peer)
            pass_on(u, B1, (upper, ax, y, c), y_peer)
            pass_on(u, D0, (every, ax, y, c), core_peer)

        def step_b(u):
            sends[u, B0].wait_recv()
            pass_on(u, C0, (lower, both, y, c), y_peer)
            sends[u, B1].wait_recv()
            pass_on(u, C1, (upper, ax, both, c), x_peer)
            pass_on(u, D0 + 1, (lower, 1 - ax, y, c), core_peer)
            pass_on(u, D0 + 2, (upper, ax, 1 - y, c), core_peer)

        def step_c(u):
            sends[u, C0].wait_recv()
            pass_on(u, D0 + 3, (lower, both, 1 - y, c), core_peer)
            sends[u, C1].wait_recv()
            pass_on(u, D0 + 4, (upper, 1 - ax, both, c), core_peer)

        def step_d(u):
            for n in range(5):
                sends[u, D0 + n].wait_recv()

        def arrive(i):
            if i + 3 < units:
                step_a(i + 3)
            if i + 2 < units:
                step_b(i + 2)
            if i + 1 < units:
                step_c(i + 1)
            if i == units - 2:
                swap_dy.start()
            step_d(i)

        def warm_up():
            step_a(0)
            step_a(1)
            step_b(0)
            step_a(2)
            step_b(1)
            step_c(0)
    else:
        def arrive(i):
            if i == units - 2:
                swap_dy.start()
            own[i].wait()

        def warm_up():
            pass

    def columns(u, at):
        return w[u, :, :, :, :, :, at].reshape(width, CHUNK)

    def row_block(u, i):
        return w[u, i].reshape(CHUNK, width)

    def chunk(i):
        return pl.ds(pl.multiple_of(i * CHUNK, CHUNK), CHUNK)

    def tile(i):
        return pl.ds(pl.multiple_of(i * TILE, TILE), TILE)

    def project(u, dst, bias, scale):
        @pl.loop(0, width // CHUNK)
        def _(i):
            at = chunk(i)
            value = dot_nn(x[...], columns(u, at))
            if bias is not None:
                value = value + par[bias : bias + 1, at]
            if scale is not None:
                value = value * scale
            dst[:, at] = value.astype(BF16)

    lane = lax.broadcasted_iota(jnp.int32, (BLOCK, PAIR), 1)
    low_half = lane < PAIR // 2
    row_lane = lax.broadcasted_iota(jnp.int32, (1, PAIR), 1)
    first_head = jnp.where(row_lane < PAIR // 2, 1.0, 0.0).astype(BF16)
    second_head = jnp.where(row_lane < PAIR // 2, 0.0, 1.0).astype(BF16)

    def heads(value):
        return jnp.concatenate([value * first_head, value * second_head], axis=0)

    def merged(value):
        return jnp.where(low_half, value[:BLOCK], value[BLOCK:])

    def softmax(scores, usable):
        scores = jnp.where(usable, scores, MASKED)
        weight = jnp.exp(scores - jnp.max(scores, axis=1, keepdims=True))
        return weight * (1.0 / jnp.sum(weight, axis=1, keepdims=True))

    pairs = width // PAIR
    key_lane = lax.broadcasted_iota(jnp.int32, (2 * BLOCK, BLOCK), 1)
    own_rows = pl.ds(short_rows, 2 * BLOCK)

    def pair_at(h):
        return slice(h * PAIR, (h + 1) * PAIR)

    def short_forward(s):
        rows = pl.ds(pl.multiple_of(s * BLOCK, BLOCK), BLOCK)
        usable = key_lane < short_len[s]
        for h in range(pairs):
            at = pair_at(h)
            p = softmax(dot_nt(heads(q[rows, at]), k[rows, at]), usable)
            g[rows, at] = merged(dot_nn(p.astype(BF16), v[rows, at])).astype(BF16)

    def long_usable():
        lanes = lax.broadcasted_iota(jnp.int32, (2 * BLOCK, 4 * BLOCK), 1)
        block = lanes // BLOCK
        inside = lanes - block * BLOCK
        mine = (2 * block + c) * BLOCK + inside
        other = (2 * (block - 2) + 1 - c) * BLOCK + inside
        return jnp.where(block < 2, mine, other) < long_len[y]

    def long_pair(h):
        return pl.ds(pl.multiple_of(h * PAIR, PAIR), PAIR)

    def long_softmax(qm, at, usable):
        scores = jnp.concatenate([dot_nt(qm, k[own_rows, at]), dot_nt(qm, kv_sib[0, :, at])], axis=1)
        return softmax(scores, usable)

    def long_forward(h):
        at = long_pair(h)
        usable = long_usable()
        for n in range(2):
            rows = pl.ds(short_rows + n * BLOCK, BLOCK)
            p = long_softmax(heads(q[rows, at]), at, usable).astype(BF16)
            o2 = dot_nn(p[:, : 2 * BLOCK], v[own_rows, at]) + dot_nn(p[:, 2 * BLOCK :], kv_sib[1, :, at])
            g[rows, at] = merged(o2).astype(BF16)

    def norm_parts(value):
        center = value - jnp.mean(value, axis=1, keepdims=True)
        scale = lax.rsqrt(jnp.mean(center * center, axis=1, keepdims=True) + EPSILON)
        return center * scale, scale

    def norm_back(grad, gain, normed, scale):
        grad = grad * gain
        return scale * (
            grad - jnp.mean(grad, axis=1, keepdims=True) - normed * jnp.mean(grad * normed, axis=1, keepdims=True))

    def row_sum(value):
        return jnp.sum(value, axis=0, keepdims=True)

    def add_sum(row, at, value):
        acc[0, row : row + 1, at] += row_sum(value)

    acc[...] = jnp.zeros_like(acc)
    for cp in loads:
        cp.wait()
    warm_up()
    arrive(K_UNIT)
    swap_x.wait_recv()
    project(K_UNIT, k, None, None)
    arrive(V_UNIT)
    project(V_UNIT, v, V_BIAS, None)
    swap_k = misc(2, k.at[own_rows], kv_sib.at[0], core_peer)
    swap_v = misc(3, v.at[own_rows], kv_sib.at[1], core_peer)
    arrive(Q_UNIT)
    swap_k.start()
    swap_v.start()
    project(Q_UNIT, q, Q_BIAS, SCALE)

    @pl.loop(0, nshort)
    def _(s):
        short_forward(s)

    swap_k.wait_recv()
    swap_v.wait_recv()

    @pl.loop(0, pairs)
    def _(h):
        long_forward(h)

    swap_k.wait_send()
    swap_v.wait_send()
    arrive(O_UNIT)

    @pl.loop(0, width // CHUNK)
    def _(i):
        at = chunk(i)
        r[:, at] = x[:, at].astype(F32) + dot_nn(g[...], columns(O_UNIT, at)) + par[O_BIAS : O_BIAS + 1, at]

    @pl.loop(0, total // TILE)
    def _(i):
        rows = tile(i)
        normed, _ = norm_parts(r[rows, :])
        value = normed * par[GAIN1 : GAIN1 + 1, :] + par[SHIFT1 : SHIFT1 + 1, :]
        a16[rows, :] = value.astype(BF16)
        f[rows, :] = value + par[D_BIAS : D_BIAS + 1, :]

    for j in range(hidden_chunks):
        up, down = UP_UNIT + 2 * j, UP_UNIT + 2 * j + 1
        arrive(up)

        @pl.loop(0, width // CHUNK)
        def _(i):
            at = chunk(i)
            value = dot_nn(a16[...], columns(up, at)) + par[U_BIAS + j : U_BIAS + j + 1, at]
            u16[j, :, at] = value.astype(BF16)
            g[:, at] = gelu(value).astype(BF16)

        if j == hidden_chunks - 2:
            for cp in late:
                cp.start()
        arrive(down)

        @pl.loop(0, width // CHUNK)
        def _(i):
            at = chunk(i)
            f[:, at] += dot_nn(g[...], columns(down, at))

    for cp in late:
        cp.wait()
    swap_dy.wait_recv()

    @pl.loop(0, total // TILE)
    def _(i):
        rows = tile(i)
        normed, scale = norm_parts(f[rows, :])
        upstream = dy[rows, :].astype(F32)
        dy[rows, :] = (normed * par[GAIN2 : GAIN2 + 1, :] + par[SHIFT2 : SHIFT2 + 1, :]).astype(BF16)
        grad = norm_back(upstream, par[GAIN2 : GAIN2 + 1, :], normed, scale)
        f[rows, :] = grad
        a16[rows, :] = grad.astype(BF16)
        add_sum(S_SUM, slice(None), upstream)
        add_sum(D_SUM, slice(None), grad)

    @pl.loop(0, hidden_chunks * (width // CHUNK))
    def _(n):
        j = n // (width // CHUNK)
        i = n % (width // CHUNK)
        at = chunk(i)
        value = dot_nt(a16[...], row_block(UP_UNIT + 1 + 2 * j, i)) * gelu_slope(u16[j, :, at].astype(F32))
        u16[j, :, at] = value.astype(BF16)
        acc[0, pl.ds(U_SUM + j, 1), at] += row_sum(value)

    out_copies = [
        pltpu.make_async_copy(dy.at[pl.ds(0, short_rows)], so, store_sem.at[0]),
        pltpu.make_async_copy(dy.at[pl.ds(short_rows + BLOCK * y, BLOCK)], lo.at[y], store_sem.at[1]),
    ]
    for cp in out_copies:
        cp.start()
    swap_out = misc(4, dy.at[pl.ds(short_rows + BLOCK * (1 - y), BLOCK)], lo.at[y], y_peer)
    swap_out.start()

    @pl.loop(0, width // CHUNK)
    def _(i):
        at = chunk(i)
        value = f[:, at]
        for j in range(hidden_chunks):
            value = value + dot_nt(u16[j], row_block(UP_UNIT + 2 * j, i))
        f[:, at] = value

    @pl.loop(0, total // TILE)
    def _(i):
        rows = tile(i)
        normed, scale = norm_parts(r[rows, :])
        upstream = f[rows, :]
        grad = norm_back(upstream, par[GAIN1 : GAIN1 + 1, :], normed, scale)
        r[rows, :] = grad
        a16[rows, :] = grad.astype(BF16)
        add_sum(F_SUM, slice(None), upstream)
        add_sum(O_SUM, slice(None), grad)

    @pl.loop(0, width // CHUNK)
    def _(i):
        at = chunk(i)
        g[:, at] = dot_nt(a16[...], row_block(O_UNIT, i)).astype(BF16)

    @pl.loop(0, pairs)
    def _(h):
        at = long_pair(h)
        usable = long_usable()
        key_own = key_other = value_own = value_other = 0.0
        query_sum = 0.0
        for n in range(2):
            rows = pl.ds(short_rows + n * BLOCK, BLOCK)
            qm = heads(q[rows, at])
            om = heads(g[rows, at])
            p = long_softmax(qm, at, usable)
            back = jnp.concatenate([dot_nt(om, v[own_rows, at]), dot_nt(om, kv_sib[1, :, at])], axis=1)
            ds = (p * (back - jnp.sum(back * p, axis=1, keepdims=True))).astype(BF16)
            low = p.astype(BF16)
            dq = merged(dot_nn(ds[:, : 2 * BLOCK], k[own_rows, at]) + dot_nn(ds[:, 2 * BLOCK :], kv_sib[0, :, at]))
            dq = dq * SCALE
            q[rows, at] = dq.astype(BF16)
            query_sum = query_sum + row_sum(dq)
            key_own = key_own + dot_tn(ds[:, : 2 * BLOCK], qm)
            key_other = key_other + dot_tn(ds[:, 2 * BLOCK :], qm)
            value_own = value_own + dot_tn(low[:, : 2 * BLOCK], om)
            value_other = value_other + dot_tn(low[:, 2 * BLOCK :], om)
        k[own_rows, at] = key_own.astype(BF16)
        v[own_rows, at] = value_own.astype(BF16)
        kv_sib[0, :, at] = key_other.astype(BF16)
        kv_sib[1, :, at] = value_other.astype(BF16)
        acc[0, Q_SUM : Q_SUM + 1, at] += query_sum
        acc[0, V_SUM : V_SUM + 1, at] += row_sum(value_own) + row_sum(value_other)

    def short_backward(s):
        rows = pl.ds(pl.multiple_of(s * BLOCK, BLOCK), BLOCK)
        usable = key_lane < short_len[s]
        for h in range(pairs):
            at = pair_at(h)
            qm = heads(q[rows, at])
            om = heads(g[rows, at])
            p = softmax(dot_nt(qm, k[rows, at]), usable)
            back = dot_nt(om, v[rows, at])
            ds = (p * (back - jnp.sum(back * p, axis=1, keepdims=True))).astype(BF16)
            dq = merged(dot_nn(ds, k[rows, at])) * SCALE
            dk = dot_tn(ds, qm)
            dv = dot_tn(p.astype(BF16), om)
            q[rows, at] = dq.astype(BF16)
            k[rows, at] = dk.astype(BF16)
            v[rows, at] = dv.astype(BF16)
            add_sum(Q_SUM, at, dq)
            add_sum(V_SUM, at, dv)

    @pl.loop(0, 1)
    def _(s):
        short_backward(s)

    swap_dkv = misc(5, kv_sib, dkv_in, core_peer)
    swap_dkv.start()

    @pl.loop(1, nshort)
    def _(s):
        short_backward(s)

    swap_dkv.wait_recv()
    k[own_rows, :] = (k[own_rows, :].astype(F32) + dkv_in[0].astype(F32)).astype(BF16)
    v[own_rows, :] = (v[own_rows, :].astype(F32) + dkv_in[1].astype(F32)).astype(BF16)

    def exchange(n):
        return misc(8 + n, acc.at[n], acc_in.at[n], partners[n])

    @pl.loop(0, width // CHUNK)
    def _(i):
        at = chunk(i)
        value = r[:, at]
        for ref, u in ((q, Q_UNIT), (k, K_UNIT), (v, V_UNIT)):
            value = value + dot_nt(ref[...], row_block(u, i))
        x[:, at] = value.astype(BF16)

    for n in range(len(partners)):
        cp = exchange(n)
        cp.start()
        cp.wait_recv()
        cp.wait_send()
        acc[n + 1] = acc[n] + acc_in[n]
    sums[...] = acc[len(partners)]

    grad_copies = [
        pltpu.make_async_copy(x.at[pl.ds(0, short_rows)], sg, store_sem.at[2]),
        pltpu.make_async_copy(x.at[pl.ds(short_rows + BLOCK * y, BLOCK)], lg.at[y], store_sem.at[3]),
    ]
    for cp in grad_copies:
        cp.start()
    swap_grad = misc(6, x.at[pl.ds(short_rows + BLOCK * (1 - y), BLOCK)], lg.at[y], y_peer)
    swap_grad.start()
    swap_out.wait_recv()
    swap_grad.wait_recv()
    for cp in out_copies + grad_copies:
        cp.wait()
    for cp in (swap_x, swap_dy, swap_out, swap_dkv, swap_grad):
        cp.wait_send()
    for key in sends:
        sends[key].wait_send()


def whole_step(wsh, xs, xl, dys, dyl, short_len, long_len, par, remote):
    dp_size, seq_size = lax.axis_size("dp"), lax.axis_size("seq")
    width = xs.shape[1]
    nshort = xs.shape[0] // BLOCK
    total = xs.shape[0] + xl.shape[0] * BLOCK
    units = wsh.shape[0]
    lead = (width // CHUNK, 2, 2, 2, CHUNK // 8, width)
    hidden_chunks = (units - 4) // 2
    slots = lead[0] + 8
    steps = (dp_size * seq_size).bit_length() - 1
    anywhere = pl.BlockSpec(memory_space=pl.ANY)
    smem = pl.BlockSpec(memory_space=pltpu.SMEM)
    vmem = pl.BlockSpec(memory_space=pltpu.VMEM)
    act = pltpu.VMEM((total, width), BF16)
    wide = pltpu.VMEM((total, width), F32)
    side = pltpu.VMEM((2, 2 * BLOCK, width), BF16)
    dma = pltpu.SemaphoreType.DMA
    return pl.pallas_call(
        functools.partial(step_kernel, remote, dp_size, seq_size, nshort),
        out_shape=(
            jax.ShapeDtypeStruct(xs.shape, BF16),
            jax.ShapeDtypeStruct(xl.shape, BF16),
            jax.ShapeDtypeStruct(xs.shape, BF16),
            jax.ShapeDtypeStruct(xl.shape, BF16),
            jax.ShapeDtypeStruct((SUMS, width), F32),
        ),
        in_specs=[anywhere] * 5 + [smem] * 2 + [vmem],
        out_specs=(anywhere,) * 4 + (vmem,),
        scratch_shapes=[
            pltpu.VMEM((units, *lead), BF16),
            act, act, act, act, side, side, act, wide, act,
            pltpu.VMEM((hidden_chunks, total, width), BF16),
            wide, act,
            pltpu.VMEM((steps + 1, SUMS, width), F32),
            pltpu.VMEM((steps, SUMS, width), F32),
            dma((units, slots)), dma((units, slots)), dma((8 + steps,)), dma((8 + steps,)),
            dma((units,)), dma((4,)), dma((4,)),
        ],
        compiler_params=pltpu.CompilerParams(
            collective_id=0, has_side_effects=True, vmem_limit_bytes=67043328),
        name="whole_step",
    )(wsh, xs, xl, dys, dyl, short_len, long_len, par)


def on_device(
    short_input, long_input, short_cotangent, long_cotangent, short_lengths, long_lengths,
    query_weight, key_weight, value_weight, output_weight, upward_weight, downward_weight,
    query_bias, value_bias, output_bias, upward_bias, downward_bias,
    first_gain, first_shift, second_gain, second_shift,
):
    rows, width = query_weight.shape
    devices = lax.axis_size("dp") * lax.axis_size("seq")
    hidden_chunks = upward_weight.shape[1] // width
    shape = short_input.shape

    def permuted(value):
        lead = value.shape[:-1]
        value = value.reshape(*lead, devices, hidden_chunks, rows)
        return jnp.moveaxis(value, -2, 0).reshape(hidden_chunks, *lead, width)

    upward = permuted(upward_weight)
    downward = downward_weight.reshape(hidden_chunks, rows, width)
    parts = [key_weight, value_weight, query_weight, output_weight]
    for j in range(hidden_chunks):
        parts += [upward[j], downward[j]]
    wsh = jnp.stack([part.astype(BF16) for part in parts])
    remote = rows == 32 and lax.axis_size("seq") == 4
    if not remote:
        wsh = lax.all_gather(wsh, ("dp", "seq"), axis=1, tiled=True)
        wsh = wsh.reshape(len(parts), width // CHUNK, 2, 2, 2, CHUNK // 8, width)
    par = jnp.concatenate([
        jnp.stack([query_bias, value_bias, output_bias, downward_bias,
                   first_gain, first_shift, second_gain, second_shift]),
        permuted(upward_bias)])
    so, lo, sg, lg, sums = whole_step(
        wsh, short_input.reshape(-1, width), long_input, short_cotangent.reshape(-1, width), long_cotangent,
        short_lengths, long_lengths, par, remote)
    upward_delta = sums[U_SUM : U_SUM + hidden_chunks].reshape(hidden_chunks, devices, rows)
    upward_delta = jnp.moveaxis(upward_delta, 0, 1).reshape(-1)
    return (
        so.reshape(shape), lo, sg.reshape(shape), lg,
        sums[Q_SUM], sums[V_SUM], sums[O_SUM], upward_delta, sums[D_SUM], sums[F_SUM], sums[S_SUM],
    )


def solution(mesh):
    split = ("dp", "seq")
    placed = (
        P(split, None, None), P("dp", "seq", None), P(split, None, None), P("dp", "seq", None),
        P(split), P("dp"),
        *(P(split, None) for _ in range(6)), *(P() for _ in range(9)),
    )
    return jax.shard_map(
        on_device,
        mesh=mesh,
        in_specs=placed,
        out_specs=(
            P(split, None, None), P("dp", "seq", None), P(split, None, None), P("dp", "seq", None),
            *(P() for _ in range(7)),
        ),
        check_vma=False,
    )
```

time: 704 us -> 264 us (0.38); the launches traced: 695 us -> 264 us
  waiting for transfers between devices: 360 us -> 0 us
  Pallas kernels: 0 us -> 247 us
  matrix products: 211 us -> 0 us
  blocking collectives: 40.4 us -> 0 us
  other arithmetic: 33 us -> 1.13 us
  local copies, waits for them, and re-layouts: 34.1 us -> 14.7 us
  between operations: 15.4 us -> 0.95 us
    all_gather x8 -> x0, waiting for transfers between devices: 360 us -> none  [the longest x1 70.5 us: on_device(): lax.all_gather(downward_low, ('dp', 'seq'), axis=0, tiled=True)]
    pallas_call x0 -> x1, Pallas kernels: none -> 247 us  [whole_step(): pl.pallas_call(functools.partial(step_kernel, remote, dp_size, seq_size,...]
    dot_general x34 -> x0, matrix products: 199 us -> none  [the longest x12 70.3 us: forward_product(): return jnp.dot(left, right, preferred_element_type=jnp.float32)]
    psum x1 -> x0, blocking collectives: 40.4 us -> none  [settle_each(): return lax.psum(value, ('dp', 'seq'))]
    convert_element_type x8 -> x0, other arithmetic: 18.9 us -> none  [the longest x2 11.2 us: backprop(): score_grad = score_grad.astype(jnp.bfloat16)]
    convert_element_type x8 -> x4, local copies, waits for them, and re-layouts: 18.3 us -> 1.11 us  [on_device(): wsh = jnp.stack([part.astype(BF16) for part in parts])]
    reduce_sum x13 -> x0, other arithmetic: 13.8 us -> none  [the longest x5 7.07 us: token_total(): return jnp.sum(value, axis=(0, 1))]
    sub x2 -> x0, matrix products: 12.3 us -> none  [recompute(): attention = jax.nn.softmax(scores, axis=-1)]
  transfers between devices with their start and end apart: 10 -> 0, of which waited for: 8 -> 0; matrix products, arithmetic and copies ran while one was open for 32% -> 0% of each run, Pallas kernels for 0% -> 0%
where the time goes in v2:
time: 264 us
  Pallas kernels  247 us (94%)
  local copies, waits for them, and re-layouts  14.7 us (6%)
    pallas_call x1, Pallas kernels, whole_step(): pl.pallas_call(functools.partial(step_kernel, remote, dp_size, seq_size,...  247 us
    unnamed x47, local copies, waits for them, and re-layouts  7.62 us

profile of v2, /device:TPU:0, one launch (start us, length us, event | category | flops | bytes accessed | tf_op | source)
XLA Modules:
  0.0 263.8 jit_solution(5658822992621876994)
XLA Ops:
  0.6 1.1 convert.15
  1.7 0.8 reshape.128
  2.5 0.2 copy.38
  2.8 0.1 fusion.4
  2.9 0.3 convert_element_type.80
  3.1 0.5 copy-done.5
  3.9 0.1 copy-done.2
  4.1 0.3 convert_element_type.82
  4.4 0.3 convert_element_type.84
  4.7 0.3 convert_element_type.86
  5.0 0.9 copy-done.1
  5.9 0.1 reshape.122
  6.0 0.1 reshape.123
  6.2 1.3 concatenate.3.par
  7.5 247.1 %whole_step.1 = (bf16[768,1024]{1,0:T(8,128)(2,1)}, bf16[2,128,1024]{2,1,0:T(8,128)(2,1)}, bf16[768,1024]{1,0:T(8,128)(2,1)}, bf16[2,128,1024]{2,1,0:T(8,128)(2,1)}, f32[16,1024]{1,0:T(8,128)}) custom-call(bf16[12,32,1024]{2,1,0:T(8,128)(2,1)} %copy-done.1, bf16[768,1024]{1,0:T(8,128)(2,1)} %bitcast.60, bf16[2,128,1024]{2,1,0:T(8,128)(2,1)} %xl.1, ...), custom_call_target="tpu_custom_call" | custom-call | tf_op jit(solution)/shard_map/whole_step/pallas_call | solution.py:521
  254.5 1.7 fusion.5
  256.3 0.8 slice.72
  257.1 0.1 reshape.126
  257.2 0.7 reshape.127
  257.9 2.9 %copy.55 = bf16[6,128,1024]{2,1,0:T(8,128)(2,1)} copy(bf16[6,128,1024]{2,1,0:T(8,128)(2,1)} %bitcast.59) | data formatting | bytes 3145728
  260.9 0.8 copy.56
  261.6 1.1 copy.57
  262.8 0.3 copy-done.3
  263.0 0.8 copy.58
  (47 shorter events, 0.4 us)
Async XLA Ops:
  2.7 0.9 copy-start.5
  2.7 1.0 copy-start.6
  2.7 1.0 copy-start.7
  2.7 1.1 copy-start.8
  2.8 1.3 copy-start.2
  3.7 2.1 copy-start.9
  3.8 2.3 copy-start.10
  3.8 2.3 copy-start.11
  3.8 2.3 copy-start.12
  3.9 2.3 copy-start.13
  3.9 2.3 copy-start.14
  3.9 2.2 copy-start.15
  3.9 2.2 copy-start.16
  3.9 2.2 copy-start.17
  5.0 0.9 copy-start.1
  257.9 2.9 %copy-start.4 = (bf16[2,128,1024]{2,1,0:T(8,128)(2,1)S(1)}, bf16[2,128,1024]{2,1,0:T(8,128)(2,1)}, u32[]{:S(2)}) copy-start(bf16[2,128,1024]{2,1,0:T(8,128)(2,1)} %get-tuple-element.43) | copy-start | bytes 1572868
  257.9 3.7 %copy-start = (bf16[768,1024]{1,0:T(8,128)(2,1)S(1)}, bf16[768,1024]{1,0:T(8,128)(2,1)}, u32[]{:S(2)}) copy-start(bf16[768,1024]{1,0:T(8,128)(2,1)} %get-tuple-element.18) | copy-start | bytes 4718596
  261.6 1.4 copy-start.3

commit v3 on v2

--- a/solution.py
+++ b/solution.py
@@ -8,6 +8,12 @@
 from jax.sharding import PartitionSpec as P
 
 MESH = pl.DeviceIdType.MESH
+
+
+def phase(name, start, stop):
+    return pl.loop(start, stop)
+
+
 F32 = jnp.float32
 BF16 = jnp.bfloat16
 EPSILON = 1e-12
@@ -19,8 +25,8 @@
 TILE = 256
 K_UNIT, V_UNIT, Q_UNIT, O_UNIT, UP_UNIT = 0, 1, 2, 3, 4
 Q_BIAS, V_BIAS, O_BIAS, D_BIAS, GAIN1, SHIFT1, GAIN2, SHIFT2, U_BIAS = 0, 1, 2, 3, 4, 5, 6, 7, 8
-Q_SUM, V_SUM, O_SUM, D_SUM, F_SUM, S_SUM, U_SUM = 0, 1, 2, 3, 4, 5, 6
-SUMS = 16
+Q_SUM, V_SUM = 0, 1
+O_SUM, D_SUM, F_SUM, S_SUM, U_SUM = 0, 1, 2, 3, 4
 
 
 def dot_nn(a, b):
@@ -39,21 +45,19 @@
     return index + bit * (1 - 2 * ((index // bit) % 2))
 
 
-def gelu(u):
-    return 0.5 * u * (1.0 + jnp.tanh(0.7978845608028654 * (u + 0.044715 * (u * u * u))))
-
-
-def gelu_slope(u):
+def gelu_parts(u):
     square = u * u
     t = jnp.tanh(0.7978845608028654 * (u + 0.044715 * (u * square)))
-    return 0.5 * (1.0 + t) + 0.5 * u * (1.0 - t * t) * (0.7978845608028654 * (1.0 + 3 * 0.044715 * square))
+    half = 0.5 * (1.0 + t)
+    slope = half + 0.5 * u * (1.0 - t * t) * (0.7978845608028654 * (1.0 + 3 * 0.044715 * square))
+    return u * half, slope
 
 
 def step_kernel(
     remote, dp_size, seq_size, nshort,
     wsh, xs, xl, dys, dyl, short_len, long_len, par,
-    so, lo, sg, lg, sums,
-    w, x, q, k, v, kv_sib, dkv_in, g, r, a16, u16, f, dy, acc, acc_in,
+    so, lo, sg, lg, sums, tail_sums, parked,
+    w, x, q, k, v, kv_sib, dkv_in, g, r, a16, hid, f, dy, acc, acc_in, tail, tail_in,
     send_sem, recv_sem, misc_send, misc_recv, own_sem, load_sem, store_sem,
 ):
     dp = lax.axis_index("dp")
@@ -196,7 +200,7 @@
         return pl.ds(pl.multiple_of(i * TILE, TILE), TILE)
 
     def project(u, dst, bias, scale):
-        @pl.loop(0, width // CHUNK)
+        @phase("proj", 0, width // CHUNK)
         def _(i):
             at = chunk(i)
             value = dot_nn(x[...], columns(u, at))
@@ -220,46 +224,54 @@
 
     def softmax(scores, usable):
         scores = jnp.where(usable, scores, MASKED)
-        weight = jnp.exp(scores - jnp.max(scores, axis=1, keepdims=True))
-        return weight * (1.0 / jnp.sum(weight, axis=1, keepdims=True))
+        weight = jnp.exp(scores - jnp.max(scores, axis=0, keepdims=True))
+        return weight * (1.0 / jnp.sum(weight, axis=0, keepdims=True))
 
     pairs = width // PAIR
-    key_lane = lax.broadcasted_iota(jnp.int32, (2 * BLOCK, BLOCK), 1)
+    per_row = width // (2 * BLOCK)
     own_rows = pl.ds(short_rows, 2 * BLOCK)
 
     def pair_at(h):
         return slice(h * PAIR, (h + 1) * PAIR)
 
+    def short_kept(s, h):
+        start = (s % 4) * (pairs // per_row) + h // per_row
+        col = h % per_row * 2 * BLOCK
+        return s // 4, pl.ds(pl.multiple_of(start * BLOCK, BLOCK), BLOCK), slice(col, col + 2 * BLOCK)
+
+    def long_kept(n, h):
+        rows = pl.ds(pl.multiple_of(h // per_row * 4 * BLOCK, 4 * BLOCK), 4 * BLOCK)
+        return 2 + n, rows, pl.ds(pl.multiple_of(h % per_row * 2 * BLOCK, 2 * BLOCK), 2 * BLOCK)
+
     def short_forward(s):
         rows = pl.ds(pl.multiple_of(s * BLOCK, BLOCK), BLOCK)
-        usable = key_lane < short_len[s]
+        usable = lax.broadcasted_iota(jnp.int32, (BLOCK, 2 * BLOCK), 0) < short_len[s]
         for h in range(pairs):
             at = pair_at(h)
-            p = softmax(dot_nt(heads(q[rows, at]), k[rows, at]), usable)
-            g[rows, at] = merged(dot_nn(p.astype(BF16), v[rows, at])).astype(BF16)
+            p = softmax(dot_nt(k[rows, at], heads(q[rows, at])), usable).astype(BF16)
+            hid[short_kept(s, h)] = p
+            g[rows, at] = merged(dot_tn(p, v[rows, at])).astype(BF16)
 
     def long_usable():
-        lanes = lax.broadcasted_iota(jnp.int32, (2 * BLOCK, 4 * BLOCK), 1)
-        block = lanes // BLOCK
-        inside = lanes - block * BLOCK
-        mine = (2 * block + c) * BLOCK + inside
-        other = (2 * (block - 2) + 1 - c) * BLOCK + inside
+        key = lax.broadcasted_iota(jnp.int32, (4 * BLOCK, 2 * BLOCK), 0)
+        block = key // BLOCK
+        mine = key + (block + c) * BLOCK
+        other = key + (block - 3 - c) * BLOCK
         return jnp.where(block < 2, mine, other) < long_len[y]
 
     def long_pair(h):
         return pl.ds(pl.multiple_of(h * PAIR, PAIR), PAIR)
-
-    def long_softmax(qm, at, usable):
-        scores = jnp.concatenate([dot_nt(qm, k[own_rows, at]), dot_nt(qm, kv_sib[0, :, at])], axis=1)
-        return softmax(scores, usable)
 
     def long_forward(h):
         at = long_pair(h)
         usable = long_usable()
         for n in range(2):
             rows = pl.ds(short_rows + n * BLOCK, BLOCK)
-            p = long_softmax(heads(q[rows, at]), at, usable).astype(BF16)
-            o2 = dot_nn(p[:, : 2 * BLOCK], v[own_rows, at]) + dot_nn(p[:, 2 * BLOCK :], kv_sib[1, :, at])
+            qm = heads(q[rows, at])
+            scores = jnp.concatenate([dot_nt(k[own_rows, at], qm), dot_nt(kv_sib[0, :, at], qm)], axis=0)
+            p = softmax(scores, usable).astype(BF16)
+            hid[long_kept(n, h)] = p
+            o2 = dot_tn(p[: 2 * BLOCK], v[own_rows, at]) + dot_tn(p[2 * BLOCK :], kv_sib[1, :, at])
             g[rows, at] = merged(o2).astype(BF16)
 
     def norm_parts(value):
@@ -278,7 +290,8 @@
     def add_sum(row, at, value):
         acc[0, row : row + 1, at] += row_sum(value)
 
-    acc[...] = jnp.zeros_like(acc)
+    acc[0] = jnp.zeros_like(acc[0])
+    tail[0] = jnp.zeros_like(tail[0])
     for cp in loads:
         cp.wait()
     warm_up()
@@ -294,27 +307,29 @@
     swap_v.start()
     project(Q_UNIT, q, Q_BIAS, SCALE)
 
-    @pl.loop(0, nshort)
+    @phase("sf", 0, nshort)
     def _(s):
         short_forward(s)
 
     swap_k.wait_recv()
     swap_v.wait_recv()
 
-    @pl.loop(0, pairs)
+    @phase("lf", 0, pairs)
     def _(h):
         long_forward(h)
 
     swap_k.wait_send()
     swap_v.wait_send()
+    park = pltpu.make_async_copy(hid, parked, store_sem.at[4])
+    park.start()
     arrive(O_UNIT)
 
-    @pl.loop(0, width // CHUNK)
+    @phase("wo", 0, width // CHUNK)
     def _(i):
         at = chunk(i)
         r[:, at] = x[:, at].astype(F32) + dot_nn(g[...], columns(O_UNIT, at)) + par[O_BIAS : O_BIAS + 1, at]
 
-    @pl.loop(0, total // TILE)
+    @phase("ln1", 0, total // TILE)
     def _(i):
         rows = tile(i)
         normed, _ = norm_parts(r[rows, :])
@@ -325,20 +340,23 @@
     for j in range(hidden_chunks):
         up, down = UP_UNIT + 2 * j, UP_UNIT + 2 * j + 1
         arrive(up)
-
-        @pl.loop(0, width // CHUNK)
+        if j == 0:
+            park.wait()
+
+        @phase("up", 0, width // CHUNK)
         def _(i):
             at = chunk(i)
             value = dot_nn(a16[...], columns(up, at)) + par[U_BIAS + j : U_BIAS + j + 1, at]
-            u16[j, :, at] = value.astype(BF16)
-            g[:, at] = gelu(value).astype(BF16)
+            active, slope = gelu_parts(value)
+            hid[j, :, at] = slope.astype(BF16)
+            g[:, at] = active.astype(BF16)
 
         if j == hidden_chunks - 2:
             for cp in late:
                 cp.start()
         arrive(down)
 
-        @pl.loop(0, width // CHUNK)
+        @phase("down", 0, width // CHUNK)
         def _(i):
             at = chunk(i)
             f[:, at] += dot_nn(g[...], columns(down, at))
@@ -347,7 +365,7 @@
         cp.wait()
     swap_dy.wait_recv()
 
-    @pl.loop(0, total // TILE)
+    @phase("ln2", 0, total // TILE)
     def _(i):
         rows = tile(i)
         normed, scale = norm_parts(f[rows, :])
@@ -359,15 +377,6 @@
         add_sum(S_SUM, slice(None), upstream)
         add_sum(D_SUM, slice(None), grad)
 
-    @pl.loop(0, hidden_chunks * (width // CHUNK))
-    def _(n):
-        j = n // (width // CHUNK)
-        i = n % (width // CHUNK)
-        at = chunk(i)
-        value = dot_nt(a16[...], row_block(UP_UNIT + 1 + 2 * j, i)) * gelu_slope(u16[j, :, at].astype(F32))
-        u16[j, :, at] = value.astype(BF16)
-        acc[0, pl.ds(U_SUM + j, 1), at] += row_sum(value)
-
     out_copies = [
         pltpu.make_async_copy(dy.at[pl.ds(0, short_rows)], so, store_sem.at[0]),
         pltpu.make_async_copy(dy.at[pl.ds(short_rows + BLOCK * y, BLOCK)], lo.at[y], store_sem.at[1]),
@@ -377,15 +386,27 @@
     swap_out = misc(4, dy.at[pl.ds(short_rows + BLOCK * (1 - y), BLOCK)], lo.at[y], y_peer)
     swap_out.start()
 
-    @pl.loop(0, width // CHUNK)
+    @phase("dg", 0, hidden_chunks * (width // CHUNK))
+    def _(n):
+        j = n // (width // CHUNK)
+        i = n % (width // CHUNK)
+        at = chunk(i)
+        value = dot_nt(a16[...], row_block(UP_UNIT + 1 + 2 * j, i)) * hid[j, :, at].astype(F32)
+        hid[j, :, at] = value.astype(BF16)
+        acc[0, pl.ds(U_SUM + j, 1), at] += row_sum(value)
+
+    @phase("da", 0, width // CHUNK)
     def _(i):
         at = chunk(i)
         value = f[:, at]
         for j in range(hidden_chunks):
-            value = value + dot_nt(u16[j], row_block(UP_UNIT + 2 * j, i))
+            value = value + dot_nt(hid[j], row_block(UP_UNIT + 2 * j, i))
         f[:, at] = value
 
-    @pl.loop(0, total // TILE)
+    unpark = pltpu.make_async_copy(parked, hid, store_sem.at[5])
+    unpark.start()
+
+    @phase("ln1b", 0, total // TILE)
     def _(i):
         rows = tile(i)
         normed, scale = norm_parts(r[rows, :])
@@ -396,92 +417,139 @@
         add_sum(F_SUM, slice(None), upstream)
         add_sum(O_SUM, slice(None), grad)
 
-    @pl.loop(0, width // CHUNK)
+    def early(n):
+        return misc(8 + n, acc.at[n], acc_in.at[n], partners[n])
+
+    def finish_early(n):
+        early(n).wait_recv()
+        early(n).wait_send()
+        acc[n + 1] = acc[n] + acc_in[n]
+
+    def next_early(n):
+        if n > 0:
+            finish_early(n - 1)
+        early(n).start()
+
+    next_early(0)
+
+    @phase("do", 0, width // CHUNK)
     def _(i):
         at = chunk(i)
         g[:, at] = dot_nt(a16[...], row_block(O_UNIT, i)).astype(BF16)
 
-    @pl.loop(0, pairs)
+    next_early(1)
+    unpark.wait()
+
+    @phase("lb", 0, pairs)
     def _(h):
         at = long_pair(h)
-        usable = long_usable()
-        key_own = key_other = value_own = value_other = 0.0
-        query_sum = 0.0
+        keys, values = k[own_rows, at], v[own_rows, at]
+        keys_far, values_far = kv_sib[0, :, at], kv_sib[1, :, at]
+        key_grad = value_grad = query_sum = 0.0
         for n in range(2):
             rows = pl.ds(short_rows + n * BLOCK, BLOCK)
             qm = heads(q[rows, at])
             om = heads(g[rows, at])
-            p = long_softmax(qm, at, usable)
-            back = jnp.concatenate([dot_nt(om, v[own_rows, at]), dot_nt(om, kv_sib[1, :, at])], axis=1)
-            ds = (p * (back - jnp.sum(back * p, axis=1, keepdims=True))).astype(BF16)
-            low = p.astype(BF16)
-            dq = merged(dot_nn(ds[:, : 2 * BLOCK], k[own_rows, at]) + dot_nn(ds[:, 2 * BLOCK :], kv_sib[0, :, at]))
-            dq = dq * SCALE
+            low = hid[long_kept(n, h)]
+            p = low.astype(F32)
+            back = jnp.concatenate([dot_nt(values, om), dot_nt(values_far, om)], axis=0)
+            ds = (p * (back - jnp.sum(back * p, axis=0, keepdims=True))).astype(BF16)
+            dq = merged(dot_tn(ds[: 2 * BLOCK], keys) + dot_tn(ds[2 * BLOCK :], keys_far)) * SCALE
             q[rows, at] = dq.astype(BF16)
             query_sum = query_sum + row_sum(dq)
-            key_own = key_own + dot_tn(ds[:, : 2 * BLOCK], qm)
-            key_other = key_other + dot_tn(ds[:, 2 * BLOCK :], qm)
-            value_own = value_own + dot_tn(low[:, : 2 * BLOCK], om)
-            value_other = value_other + dot_tn(low[:, 2 * BLOCK :], om)
-        k[own_rows, at] = key_own.astype(BF16)
-        v[own_rows, at] = value_own.astype(BF16)
-        kv_sib[0, :, at] = key_other.astype(BF16)
-        kv_sib[1, :, at] = value_other.astype(BF16)
-        acc[0, Q_SUM : Q_SUM + 1, at] += query_sum
-        acc[0, V_SUM : V_SUM + 1, at] += row_sum(value_own) + row_sum(value_other)
+            key_grad = key_grad + dot_nn(ds, qm)
+            value_grad = value_grad + dot_nn(low, om)
+        k[own_rows, at] = key_grad[: 2 * BLOCK].astype(BF16)
+        v[own_rows, at] = value_grad[: 2 * BLOCK].astype(BF16)
+        kv_sib[0, :, at] = key_grad[2 * BLOCK :].astype(BF16)
+        kv_sib[1, :, at] = value_grad[2 * BLOCK :].astype(BF16)
+        tail[0, Q_SUM : Q_SUM + 1, at] += query_sum
+        tail[0, V_SUM : V_SUM + 1, at] += row_sum(value_grad)
 
     def short_backward(s):
         rows = pl.ds(pl.multiple_of(s * BLOCK, BLOCK), BLOCK)
-        usable = key_lane < short_len[s]
         for h in range(pairs):
             at = pair_at(h)
             qm = heads(q[rows, at])
             om = heads(g[rows, at])
-            p = softmax(dot_nt(qm, k[rows, at]), usable)
-            back = dot_nt(om, v[rows, at])
-            ds = (p * (back - jnp.sum(back * p, axis=1, keepdims=True))).astype(BF16)
-            dq = merged(dot_nn(ds, k[rows, at])) * SCALE
-            dk = dot_tn(ds, qm)
-            dv = dot_tn(p.astype(BF16), om)
+            keys = k[rows, at]
+            low = hid[short_kept(s, h)]
+            p = low.astype(F32)
+            back = dot_nt(v[rows, at], om)
+            ds = (p * (back - jnp.sum(back * p, axis=0, keepdims=True))).astype(BF16)
+            dq = merged(dot_tn(ds, keys)) * SCALE
+            dk = dot_nn(ds, qm)
+            dv = dot_nn(low, om)
             q[rows, at] = dq.astype(BF16)
             k[rows, at] = dk.astype(BF16)
             v[rows, at] = dv.astype(BF16)
-            add_sum(Q_SUM, at, dq)
-            add_sum(V_SUM, at, dv)
-
-    @pl.loop(0, 1)
+            tail[0, Q_SUM : Q_SUM + 1, at] += row_sum(dq)
+            tail[0, V_SUM : V_SUM + 1, at] += row_sum(dv)
+
+    next_early(2)
+
+    @phase("sb1", 0, 1)
     def _(s):
         short_backward(s)
 
     swap_dkv = misc(5, kv_sib, dkv_in, core_peer)
     swap_dkv.start()
-
-    @pl.loop(1, nshort)
+    next_early(3)
+
+    @phase("sb2", 1, nshort)
     def _(s):
         short_backward(s)
 
+    steps = len(partners)
+
+    def late_sum(n):
+        return misc(8 + steps + n, tail.at[n], tail_in.at[n], partners[n])
+
+    def finish_late(n):
+        late_sum(n).wait_recv()
+        late_sum(n).wait_send()
+        tail[n + 1] = tail[n] + tail_in[n]
+
+    def next_late(n):
+        if n > 0:
+            finish_late(n - 1)
+        late_sum(n).start()
+
+    next_late(0)
+    for n in range(4, steps):
+        next_early(n)
     swap_dkv.wait_recv()
     k[own_rows, :] = (k[own_rows, :].astype(F32) + dkv_in[0].astype(F32)).astype(BF16)
     v[own_rows, :] = (v[own_rows, :].astype(F32) + dkv_in[1].astype(F32)).astype(BF16)
 
-    def exchange(n):
-        return misc(8 + n, acc.at[n], acc_in.at[n], partners[n])
-
-    @pl.loop(0, width // CHUNK)
+    def input_grad(rows, i):
+        at = chunk(i)
+        value = r[rows, at]
+        for ref, u in ((q, Q_UNIT), (k, K_UNIT), (v, V_UNIT)):
+            value = value + dot_nt(ref[rows, :], row_block(u, i))
+        x[rows, at] = value.astype(BF16)
+
+    @phase("gxl", 0, width // CHUNK)
     def _(i):
-        at = chunk(i)
-        value = r[:, at]
-        for ref, u in ((q, Q_UNIT), (k, K_UNIT), (v, V_UNIT)):
-            value = value + dot_nt(ref[...], row_block(u, i))
-        x[:, at] = value.astype(BF16)
-
-    for n in range(len(partners)):
-        cp = exchange(n)
-        cp.start()
-        cp.wait_recv()
-        cp.wait_send()
-        acc[n + 1] = acc[n] + acc_in[n]
-    sums[...] = acc[len(partners)]
+        input_grad(own_rows, i)
+
+    swap_grad = misc(6, x.at[pl.ds(short_rows + BLOCK * (1 - y), BLOCK)], lg.at[y], y_peer)
+    swap_grad.start()
+    finish_early(steps - 1)
+    next_late(1)
+    for i in range(width // CHUNK):
+
+        @phase("gxs", i, i + 1)
+        def _(n):
+            input_grad(pl.ds(0, short_rows), n)
+
+        if i + 2 < steps:
+            next_late(i + 2)
+    for n in range(width // CHUNK + 2, steps):
+        next_late(n)
+    finish_late(steps - 1)
+    sums[...] = acc[steps]
+    tail_sums[...] = tail[steps]
 
     grad_copies = [
         pltpu.make_async_copy(x.at[pl.ds(0, short_rows)], sg, store_sem.at[2]),
@@ -489,8 +557,6 @@
     ]
     for cp in grad_copies:
         cp.start()
-    swap_grad = misc(6, x.at[pl.ds(short_rows + BLOCK * (1 - y), BLOCK)], lg.at[y], y_peer)
-    swap_grad.start()
     swap_out.wait_recv()
     swap_grad.wait_recv()
     for cp in out_copies + grad_copies:
@@ -525,19 +591,23 @@
             jax.ShapeDtypeStruct(xl.shape, BF16),
             jax.ShapeDtypeStruct(xs.shape, BF16),
             jax.ShapeDtypeStruct(xl.shape, BF16),
-            jax.ShapeDtypeStruct((SUMS, width), F32),
+            jax.ShapeDtypeStruct((4 + hidden_chunks, width), F32),
+            jax.ShapeDtypeStruct((2, width), F32),
+            jax.ShapeDtypeStruct((hidden_chunks, total, width), BF16),
         ),
         in_specs=[anywhere] * 5 + [smem] * 2 + [vmem],
-        out_specs=(anywhere,) * 4 + (vmem,),
+        out_specs=(anywhere,) * 4 + (vmem,) * 2 + (anywhere,),
         scratch_shapes=[
             pltpu.VMEM((units, *lead), BF16),
             act, act, act, act, side, side, act, wide, act,
             pltpu.VMEM((hidden_chunks, total, width), BF16),
             wide, act,
-            pltpu.VMEM((steps + 1, SUMS, width), F32),
-            pltpu.VMEM((steps, SUMS, width), F32),
-            dma((units, slots)), dma((units, slots)), dma((8 + steps,)), dma((8 + steps,)),
-            dma((units,)), dma((4,)), dma((4,)),
+            pltpu.VMEM((steps + 1, 4 + hidden_chunks, width), F32),
+            pltpu.VMEM((steps, 4 + hidden_chunks, width), F32),
+            pltpu.VMEM((steps + 1, 2, width), F32),
+            pltpu.VMEM((steps, 2, width), F32),
+            dma((units, slots)), dma((units, slots)), dma((8 + 2 * steps,)), dma((8 + 2 * steps,)),
+            dma((units,)), dma((4,)), dma((6,)),
         ],
         compiler_params=pltpu.CompilerParams(
             collective_id=0, has_side_effects=True, vmem_limit_bytes=67043328),
@@ -575,14 +645,14 @@
         jnp.stack([query_bias, value_bias, output_bias, downward_bias,
                    first_gain, first_shift, second_gain, second_shift]),
         permuted(upward_bias)])
-    so, lo, sg, lg, sums = whole_step(
+    so, lo, sg, lg, sums, tail_sums, _ = whole_step(
         wsh, short_input.reshape(-1, width), long_input, short_cotangent.reshape(-1, width), long_cotangent,
         short_lengths, long_lengths, par, remote)
     upward_delta = sums[U_SUM : U_SUM + hidden_chunks].reshape(hidden_chunks, devices, rows)
     upward_delta = jnp.moveaxis(upward_delta, 0, 1).reshape(-1)
     return (
         so.reshape(shape), lo, sg.reshape(shape), lg,
-        sums[Q_SUM], sums[V_SUM], sums[O_SUM], upward_delta, sums[D_SUM], sums[F_SUM], sums[S_SUM],
+        tail_sums[Q_SUM], tail_sums[V_SUM], sums[O_SUM], upward_delta, sums[D_SUM], sums[F_SUM], sums[S_SUM],
     )
 
 

time: 264 us -> 242 us (0.917)
  Pallas kernels: 247 us -> 218 us
  local copies, waits for them, and re-layouts: 14.7 us -> 19.4 us
    pallas_call x1, Pallas kernels: 247 us -> 218 us  [whole_step(): pl.pallas_call(functools.partial(step_kernel, remote, dp_size, seq_size,...]
    unnamed x47 -> x27, local copies, waits for them, and re-layouts: 7.62 us -> 10.4 us
where the time goes in v3:
time: 242 us
  Pallas kernels  218 us (90%)
  local copies, waits for them, and re-layouts  19.4 us (8%)
  other arithmetic  3.65 us (2%)
    pallas_call x1, Pallas kernels, whole_step(): pl.pallas_call(functools.partial(step_kernel, remote, dp_size, seq_size,...  218 us
    unnamed x27, local copies, waits for them, and re-layouts  10.4 us

profile of v3, /device:TPU:0, one launch (start us, length us, event | category | flops | bytes accessed | tf_op | source)
XLA Modules:
  0.0 241.8 jit_solution(12818419263811468479)
XLA Ops:
  0.7 0.9 reshape.122
  1.6 2.1 concatenate.3.par
  3.7 1.1 convert.13
  4.9 0.8 reshape.128
  7.1 0.6 bitcast_dynamic-update-slice_fusion.3
  7.8 0.6 bitcast_dynamic-update-slice_fusion.2
  8.4 0.6 bitcast_dynamic-update-slice_fusion.1
  9.0 0.6 bitcast_dynamic-update-slice_fusion
  9.7 0.6 constant_dynamic-update-slice_fusion.3
  10.3 0.6 fusion.3
  10.9 0.6 constant_dynamic-update-slice_fusion.2
  11.6 0.6 fusion.2
  12.2 0.6 constant_dynamic-update-slice_fusion.1
  12.8 0.6 fusion.1
  13.5 0.6 constant_dynamic-update-slice_fusion
  14.1 0.6 fusion.wsh
  14.7 218.0 %whole_step.1 = (bf16[768,1024]{1,0:T(8,128)(2,1)}, bf16[2,128,1024]{2,1,0:T(8,128)(2,1)}, bf16[768,1024]{1,0:T(8,128)(2,1)}, bf16[2,128,1024]{2,1,0:T(8,128)(2,...) custom-call(bf16[12,32,1024]{2,1,0:T(8,128)(2,1)} %fusion.wsh, ...), custom_call_target="tpu_custom_call" | custom-call | tf_op jit(solution)/shard_map/whole_step/pallas_call | solution.py:587
  232.7 0.8 slice.72
  233.5 1.6 fusion.5
  235.2 0.7 reshape.127
  235.9 2.9 %copy.55 = bf16[6,128,1024]{2,1,0:T(8,128)(2,1)} copy(bf16[6,128,1024]{2,1,0:T(8,128)(2,1)} %bitcast.59) | data formatting | bytes 3145728
  238.8 0.8 copy.56
  239.6 1.1 copy.57
  241.0 0.8 copy.58
  (27 shorter events, 1.9 us)
Async XLA Ops:
  0.6 4.2 %copy-start.1 = (f32[32,4096]{1,0:T(8,128)S(1)}, f32[32,4096]{1,0:T(8,128)}, u32[]{:S(2)}) copy-start(f32[32,4096]{1,0:T(8,128)} %param.31) | copy-start | bytes 1572868
  5.8 1.3 copy-start.4
  5.9 1.9 copy-start.5
  5.9 2.5 %copy-start.6 = (f32[32,1024]{1,0:T(8,128)S(1)}, f32[32,1024]{1,0:T(8,128)}, u32[]{:S(2)}) copy-start(f32[32,1024]{1,0:T(8,128)} %param.27) | copy-start | bytes 393220
  5.9 3.2 %copy-start.7 = (f32[32,1024]{1,0:T(8,128)S(1)}, f32[32,1024]{1,0:T(8,128)}, u32[]{:S(2)}) copy-start(f32[32,1024]{1,0:T(8,128)} %param.30) | copy-start | bytes 393220
  235.9 2.9 %copy-start.3 = (bf16[2,128,1024]{2,1,0:T(8,128)(2,1)S(1)}, bf16[2,128,1024]{2,1,0:T(8,128)(2,1)}, u32[]{:S(2)}) copy-start(bf16[2,128,1024]{2,1,0:T(8,128)(2,1)} %get-tuple-element.47) | copy-start | bytes 1572868
  235.9 3.7 %copy-start = (bf16[768,1024]{1,0:T(8,128)(2,1)S(1)}, bf16[768,1024]{1,0:T(8,128)(2,1)}, u32[]{:S(2)}) copy-start(bf16[768,1024]{1,0:T(8,128)(2,1)} %get-tuple-element.19) | copy-start | bytes 4718596
  239.6 1.4 copy-start.2

commit v4 on v3

--- a/solution.py
+++ b/solution.py
@@ -53,13 +53,26 @@
     return u * half, slope
 
 
+def every_fourth(pieces, j, lanes, stride):
+    found = []
+    for piece in pieces:
+        for start in range(j * lanes, piece.shape[1], stride * lanes):
+            found.append(piece[:, start : start + lanes])
+    return found
+
+
 def step_kernel(
     remote, dp_size, seq_size, nshort,
-    wsh, xs, xl, dys, dyl, short_len, long_len, par,
-    so, lo, sg, lg, sums, tail_sums, parked,
-    w, x, q, k, v, kv_sib, dkv_in, g, r, a16, hid, f, dy, acc, acc_in, tail, tail_in,
-    send_sem, recv_sem, misc_send, misc_recv, own_sem, load_sem, store_sem,
+    *refs,
 ):
+    given = 6 if remote else 1
+    shards, refs = refs[:given], refs[given:]
+    small, refs = refs[:9], refs[9:]
+    (xs, xl, dys, dyl, short_len, long_len,
+     so, lo, sg, lg, sums, up_sums, parked,
+     par, wide_par,
+     w, x, q, k, v, kv_sib, dkv_in, g, r, a16, hid, f, dy, acc, acc_in, tail, tail_in,
+     send_sem, recv_sem, misc_send, misc_recv, own_sem, small_sem, load_sem, store_sem) = refs
     dp = lax.axis_index("dp")
     seq = lax.axis_index("seq")
     y, c = seq // 2, seq % 2
@@ -93,16 +106,38 @@
         z_peers = [((z + n) % depth * 2 + ax, seq) for n in range(1, depth)]
         x_peer = (flipped(dp, 1), seq)
         peers = z_peers + [x_peer, y_peer, core_peer]
-        own = [pltpu.make_async_copy(wsh.at[u], w.at[u, z, ax, y, c], own_sem.at[u]) for u in range(units)]
+        piece = w.shape[5]
+        key_shard, value_shard, query_shard, output_shard, up_shard, down_shard = shards
+        sources = [key_shard, value_shard, query_shard, output_shard]
+        sources += [up_shard.at[:, pl.ds(n * width, width)] for n in range(hidden_chunks)]
+        sources += [down_shard.at[pl.ds(n * piece, piece)] for n in range(hidden_chunks)]
+        own = [pltpu.make_async_copy(source, f.at[pl.ds(n * piece, piece)], own_sem.at[n])
+               for n, source in enumerate(sources)]
     else:
         peers = partners
-        own = [pltpu.make_async_copy(wsh.at[u], w.at[u], own_sem.at[u]) for u in range(units)]
+        own = [pltpu.make_async_copy(shards[0].at[u], w.at[u], own_sem.at[u]) for u in range(units)]
     for cp in own:
+        cp.start()
+    small_loads = [pltpu.make_async_copy(ref, par.at[n] if n < U_BIAS else wide_par, small_sem.at[n])
+                   for n, ref in enumerate(small)]
+    for cp in small_loads:
         cp.start()
 
     barrier = pltpu.get_barrier_semaphore()
     for peer in peers:
         pl.semaphore_signal(barrier, inc=1, device_id=peer, device_id_type=MESH)
+
+    if remote:
+        lanes = width // (8 * depth)
+        for cp in own:
+            cp.wait()
+        for u in range(4):
+            w[u, z, ax, y, c] = f[u * piece : (u + 1) * piece, :].astype(BF16)
+        up_rows = [f[(4 + n) * piece : (5 + n) * piece, :].astype(BF16) for n in range(hidden_chunks)]
+        for j in range(hidden_chunks):
+            first = (4 + hidden_chunks + j) * piece
+            w[UP_UNIT + 2 * j, z, ax, y, c] = jnp.concatenate(every_fourth(up_rows, j, lanes, hidden_chunks), axis=1)
+            w[UP_UNIT + 2 * j + 1, z, ax, y, c] = f[first : first + piece, :].astype(BF16)
     pl.semaphore_wait(barrier, len(peers))
 
     def misc(slot, src, dst, peer):
@@ -132,12 +167,11 @@
 
         for u in range(units):
             for n in range(hops):
-                send(u, n, wsh.at[u], (z, ax, y, c), z_peers[n])
+                pass_on(u, n, (z, ax, y, c), z_peers[n])
 
         def step_a(u):
             for n in range(hops):
                 sends[u, n].wait_recv()
-            own[u].wait()
             pass_on(u, B0, (lower, ax, y, c), x_peer)
             pass_on(u, B1, (upper, ax, y, c), y_peer)
             pass_on(u, D0, (every, ax, y, c), core_peer)
@@ -205,7 +239,7 @@
             at = chunk(i)
             value = dot_nn(x[...], columns(u, at))
             if bias is not None:
-                value = value + par[bias : bias + 1, at]
+                value = value + par[bias, :, at]
             if scale is not None:
                 value = value * scale
             dst[:, at] = value.astype(BF16)
@@ -292,6 +326,13 @@
 
     acc[0] = jnp.zeros_like(acc[0])
     tail[0] = jnp.zeros_like(tail[0])
+    for cp in small_loads:
+        cp.wait()
+    for j in range(hidden_chunks):
+        if remote:
+            par[U_BIAS + j] = jnp.concatenate(every_fourth([wide_par[...]], j, lanes, hidden_chunks), axis=1)
+        else:
+            par[U_BIAS + j] = wide_par[:, j * width : (j + 1) * width]
     for cp in loads:
         cp.wait()
     warm_up()
@@ -307,10 +348,17 @@
     swap_v.start()
     project(Q_UNIT, q, Q_BIAS, SCALE)
 
-    @phase("sf", 0, nshort)
+    @phase("sf", 0, nshort // 2)
     def _(s):
         short_forward(s)
 
+    arrive(O_UNIT)
+
+    @phase("sf2", nshort // 2, nshort)
+    def _(s):
+        short_forward(s)
+
+    arrive(UP_UNIT)
     swap_k.wait_recv()
     swap_v.wait_recv()
 
@@ -322,31 +370,33 @@
     swap_v.wait_send()
     park = pltpu.make_async_copy(hid, parked, store_sem.at[4])
     park.start()
-    arrive(O_UNIT)
+    arrive(UP_UNIT + 1)
 
     @phase("wo", 0, width // CHUNK)
     def _(i):
         at = chunk(i)
-        r[:, at] = x[:, at].astype(F32) + dot_nn(g[...], columns(O_UNIT, at)) + par[O_BIAS : O_BIAS + 1, at]
+        r[:, at] = x[:, at].astype(F32) + dot_nn(g[...], columns(O_UNIT, at)) + par[O_BIAS, :, at]
 
     @phase("ln1", 0, total // TILE)
     def _(i):
         rows = tile(i)
         normed, _ = norm_parts(r[rows, :])
-        value = normed * par[GAIN1 : GAIN1 + 1, :] + par[SHIFT1 : SHIFT1 + 1, :]
+        value = normed * par[GAIN1] + par[SHIFT1]
         a16[rows, :] = value.astype(BF16)
-        f[rows, :] = value + par[D_BIAS : D_BIAS + 1, :]
-
+        f[rows, :] = value + par[D_BIAS]
+
+    park.wait()
     for j in range(hidden_chunks):
         up, down = UP_UNIT + 2 * j, UP_UNIT + 2 * j + 1
-        arrive(up)
         if j == 0:
-            park.wait()
+            arrive(down + 1)
+        elif j > 1:
+            arrive(up)
 
         @phase("up", 0, width // CHUNK)
         def _(i):
             at = chunk(i)
-            value = dot_nn(a16[...], columns(up, at)) + par[U_BIAS + j : U_BIAS + j + 1, at]
+            value = dot_nn(a16[...], columns(up, at)) + par[U_BIAS + j, :, at]
             active, slope = gelu_parts(value)
             hid[j, :, at] = slope.astype(BF16)
             g[:, at] = active.astype(BF16)
@@ -354,7 +404,8 @@
         if j == hidden_chunks - 2:
             for cp in late:
                 cp.start()
-        arrive(down)
+        if j > 0:
+            arrive(down)
 
         @phase("down", 0, width // CHUNK)
         def _(i):
@@ -370,8 +421,8 @@
         rows = tile(i)
         normed, scale = norm_parts(f[rows, :])
         upstream = dy[rows, :].astype(F32)
-        dy[rows, :] = (normed * par[GAIN2 : GAIN2 + 1, :] + par[SHIFT2 : SHIFT2 + 1, :]).astype(BF16)
-        grad = norm_back(upstream, par[GAIN2 : GAIN2 + 1, :], normed, scale)
+        dy[rows, :] = (normed * par[GAIN2] + par[SHIFT2]).astype(BF16)
+        grad = norm_back(upstream, par[GAIN2], normed, scale)
         f[rows, :] = grad
         a16[rows, :] = grad.astype(BF16)
         add_sum(S_SUM, slice(None), upstream)
@@ -411,7 +462,7 @@
         rows = tile(i)
         normed, scale = norm_parts(r[rows, :])
         upstream = f[rows, :]
-        grad = norm_back(upstream, par[GAIN1 : GAIN1 + 1, :], normed, scale)
+        grad = norm_back(upstream, par[GAIN1], normed, scale)
         r[rows, :] = grad
         a16[rows, :] = grad.astype(BF16)
         add_sum(F_SUM, slice(None), upstream)
@@ -548,8 +599,15 @@
     for n in range(width // CHUNK + 2, steps):
         next_late(n)
     finish_late(steps - 1)
-    sums[...] = acc[steps]
-    tail_sums[...] = tail[steps]
+    sums[0:2, :] = tail[steps]
+    sums[2:6, :] = acc[steps, 0:4, :]
+    hidden_sums = [acc[steps, U_SUM + j : U_SUM + j + 1, :] for j in range(hidden_chunks)]
+    if remote:
+        order = [hidden_sums[j][:, n * lanes : (n + 1) * lanes]
+                 for n in range(width // lanes) for j in range(hidden_chunks)]
+        up_sums[...] = jnp.concatenate(order, axis=1)
+    else:
+        up_sums[...] = jnp.concatenate(hidden_sums, axis=1)
 
     grad_copies = [
         pltpu.make_async_copy(x.at[pl.ds(0, short_rows)], sg, store_sem.at[2]),
@@ -567,14 +625,14 @@
         sends[key].wait_send()
 
 
-def whole_step(wsh, xs, xl, dys, dyl, short_len, long_len, par, remote):
+def whole_step(shards, small, xs, xl, dys, dyl, short_len, long_len, remote):
     dp_size, seq_size = lax.axis_size("dp"), lax.axis_size("seq")
     width = xs.shape[1]
     nshort = xs.shape[0] // BLOCK
     total = xs.shape[0] + xl.shape[0] * BLOCK
-    units = wsh.shape[0]
+    hidden_chunks = small[-1].shape[1] // width
+    units = 4 + 2 * hidden_chunks
     lead = (width // CHUNK, 2, 2, 2, CHUNK // 8, width)
-    hidden_chunks = (units - 4) // 2
     slots = lead[0] + 8
     steps = (dp_size * seq_size).bit_length() - 1
     anywhere = pl.BlockSpec(memory_space=pl.ANY)
@@ -591,13 +649,15 @@
             jax.ShapeDtypeStruct(xl.shape, BF16),
             jax.ShapeDtypeStruct(xs.shape, BF16),
             jax.ShapeDtypeStruct(xl.shape, BF16),
-            jax.ShapeDtypeStruct((4 + hidden_chunks, width), F32),
-            jax.ShapeDtypeStruct((2, width), F32),
+            jax.ShapeDtypeStruct((8, width), F32),
+            jax.ShapeDtypeStruct((1, hidden_chunks * width), F32),
             jax.ShapeDtypeStruct((hidden_chunks, total, width), BF16),
         ),
-        in_specs=[anywhere] * 5 + [smem] * 2 + [vmem],
+        in_specs=[anywhere] * (len(shards) + len(small) + 4) + [smem] * 2,
         out_specs=(anywhere,) * 4 + (vmem,) * 2 + (anywhere,),
         scratch_shapes=[
+            pltpu.VMEM((U_BIAS + hidden_chunks, 1, width), F32),
+            pltpu.VMEM((1, hidden_chunks * width), F32),
             pltpu.VMEM((units, *lead), BF16),
             act, act, act, act, side, side, act, wide, act,
             pltpu.VMEM((hidden_chunks, total, width), BF16),
@@ -607,12 +667,12 @@
             pltpu.VMEM((steps + 1, 2, width), F32),
             pltpu.VMEM((steps, 2, width), F32),
             dma((units, slots)), dma((units, slots)), dma((8 + 2 * steps,)), dma((8 + 2 * steps,)),
-            dma((units,)), dma((4,)), dma((6,)),
+            dma((units,)), dma((len(small),)), dma((4,)), dma((6,)),
         ],
         compiler_params=pltpu.CompilerParams(
             collective_id=0, has_side_effects=True, vmem_limit_bytes=67043328),
         name="whole_step",
-    )(wsh, xs, xl, dys, dyl, short_len, long_len, par)
+    )(*shards, *small, xs, xl, dys, dyl, short_len, long_len)
 
 
 def on_device(
@@ -631,28 +691,32 @@
         value = value.reshape(*lead, devices, hidden_chunks, rows)
         return jnp.moveaxis(value, -2, 0).reshape(hidden_chunks, *lead, width)
 
-    upward = permuted(upward_weight)
-    downward = downward_weight.reshape(hidden_chunks, rows, width)
-    parts = [key_weight, value_weight, query_weight, output_weight]
-    for j in range(hidden_chunks):
-        parts += [upward[j], downward[j]]
-    wsh = jnp.stack([part.astype(BF16) for part in parts])
     remote = rows == 32 and lax.axis_size("seq") == 4
-    if not remote:
-        wsh = lax.all_gather(wsh, ("dp", "seq"), axis=1, tiled=True)
-        wsh = wsh.reshape(len(parts), width // CHUNK, 2, 2, 2, CHUNK // 8, width)
-    par = jnp.concatenate([
-        jnp.stack([query_bias, value_bias, output_bias, downward_bias,
-                   first_gain, first_shift, second_gain, second_shift]),
-        permuted(upward_bias)])
-    so, lo, sg, lg, sums, tail_sums, _ = whole_step(
-        wsh, short_input.reshape(-1, width), long_input, short_cotangent.reshape(-1, width), long_cotangent,
-        short_lengths, long_lengths, par, remote)
-    upward_delta = sums[U_SUM : U_SUM + hidden_chunks].reshape(hidden_chunks, devices, rows)
-    upward_delta = jnp.moveaxis(upward_delta, 0, 1).reshape(-1)
+    small = [query_bias, value_bias, output_bias, downward_bias, first_gain, first_shift, second_gain, second_shift]
+    if remote:
+        shards = [key_weight, value_weight, query_weight, output_weight, upward_weight, downward_weight]
+        small.append(upward_bias)
+    else:
+        upward = permuted(upward_weight)
+        downward = downward_weight.reshape(hidden_chunks, rows, width)
+        parts = [key_weight, value_weight, query_weight, output_weight]
+        for j in range(hidden_chunks):
+            parts += [upward[j], downward[j]]
+        whole = lax.all_gather(jnp.stack([part.astype(BF16) for part in parts]), ("dp", "seq"), axis=1, tiled=True)
+        shards = [whole.reshape(len(parts), width // CHUNK, 2, 2, 2, CHUNK // 8, width)]
+        small.append(permuted(upward_bias))
+    so, lo, sg, lg, sums, up_sums, _ = whole_step(
+        shards, [value.reshape(1, -1) for value in small],
+        short_input.reshape(-1, width), long_input, short_cotangent.reshape(-1, width), long_cotangent,
+        short_lengths, long_lengths, remote)
+    if remote:
+        upward_delta = up_sums.reshape(-1)
+    else:
+        upward_delta = jnp.moveaxis(up_sums.reshape(hidden_chunks, devices, rows), 0, 1).reshape(-1)
+    query_delta, value_delta, output_delta, downward_delta, first_delta, second_delta = (sums[n] for n in range(6))
     return (
         so.reshape(shape), lo, sg.reshape(shape), lg,
-        tail_sums[Q_SUM], tail_sums[V_SUM], sums[O_SUM], upward_delta, sums[D_SUM], sums[F_SUM], sums[S_SUM],
+        query_delta, value_delta, output_delta, upward_delta, downward_delta, first_delta, second_delta,
     )
 
 

time: 242 us -> 221 us (0.913)
  local copies, waits for them, and re-layouts: 19.4 us -> 8.08 us
  Pallas kernels: 218 us -> 212 us
  other arithmetic: 3.65 us -> 0 us
    pallas_call x1, Pallas kernels: 218 us -> 212 us  [whole_step(): pl.pallas_call(functools.partial(step_kernel, remote, dp_size, seq_size,...]
    unnamed x27 -> x13, local copies, waits for them, and re-layouts: 10.4 us -> 6.48 us
    unnamed x4 -> x0, other arithmetic: 2.55 us -> none
where the time goes in v4:
time: 221 us
  Pallas kernels  212 us (96%)
  local copies, waits for them, and re-layouts  8.08 us (4%)
    pallas_call x1, Pallas kernels, whole_step(): pl.pallas_call(functools.partial(step_kernel, remote, dp_size, seq_size,...  212 us
    unnamed x13, local copies, waits for them, and re-layouts  6.48 us

profile of v4, /device:TPU:0, one launch (start us, length us, event | category | flops | bytes accessed | tf_op | source)
XLA Modules:
  0.0 221.1 jit_solution(16386664204558677238)
XLA Ops:
  0.7 212.4 %whole_step.1 = (bf16[768,1024]{1,0:T(8,128)(2,1)}, bf16[2,128,1024]{2,1,0:T(8,128)(2,1)}, bf16[768,1024]{1,0:T(8,128)(2,1)}, bf16[2,128,1024]{2,1,0:T(8,128)(2,...) custom-call(f32[32,1024]{1,0:T(8,128)} %refs_0_.1, f32[32,1024]{1,0:T(8,128)} %refs_1_.1, ...), custom_call_target="tpu_custom_call" | custom-call | tf_op jit(solution)/shard_map/whole_step/pallas_call | solution.py:645
  213.0 1.6 fusion
  214.6 0.0 copy-start.2
  214.7 0.0 copy-start
  214.7 2.9 %copy.37 = bf16[6,128,1024]{2,1,0:T(8,128)(2,1)} copy(bf16[6,128,1024]{2,1,0:T(8,128)(2,1)} %bitcast.21) | data formatting | bytes 3145728
  217.6 0.0 copy-done.2
  217.6 0.8 copy.38
  218.4 0.0 copy-done
  218.4 0.0 copy-start.1
  218.4 0.0 copy-start.3
  218.4 1.1 copy.39
  219.5 0.2 copy-done.1
  219.7 0.8 copy.40
  220.5 0.0 copy-done.3
  220.5 0.6 copy.41
Async XLA Ops:
  214.6 2.9 %copy-start.2 = (bf16[2,128,1024]{2,1,0:T(8,128)(2,1)S(1)}, bf16[2,128,1024]{2,1,0:T(8,128)(2,1)}, u32[]{:S(2)}) copy-start(bf16[2,128,1024]{2,1,0:T(8,128)(2,1)} %get-tuple-element.41) | copy-start | bytes 1572868
  214.7 3.7 %copy-start = (bf16[768,1024]{1,0:T(8,128)(2,1)S(1)}, bf16[768,1024]{1,0:T(8,128)(2,1)}, u32[]{:S(2)}) copy-start(bf16[768,1024]{1,0:T(8,128)(2,1)} %get-tuple-element.19) | copy-start | bytes 4718596
  218.4 1.4 copy-start.1
  218.4 2.2 copy-start.3

commit v5 on v4

--- a/solution.py
+++ b/solution.py
@@ -149,69 +149,112 @@
     swap_dy = misc(1, dyl.at[1 - y], dy.at[pl.ds(short_rows + BLOCK * y, BLOCK)], y_peer)
     swap_x.start()
 
-    sends = {}
+    sends, inner_sends = {}, []
     if remote:
         half = depth // 2
-        lower, upper, every, both = pl.ds(0, half), pl.ds(half, depth - half), pl.ds(0, depth), pl.ds(0, 2)
-        B0, B1, C0, C1, D0 = hops, hops + 1, hops + 2, hops + 3, hops + 4
-
-        def send(u, slot, src, part, peer):
+        lower, upper, every, both = pl.ds(0, half), pl.ds(half, half), pl.ds(0, depth), pl.ds(0, 2)
+        pair, far_pair = pl.ds(z // 2 * 2, 2), pl.ds(2 - z // 2 * 2, 2)
+        top, bottom = pl.ds(0, piece // 2), pl.ds(piece // 2, piece // 2)
+        is_inner = (z + 1) // 2 == 1
+        z_next = (flipped(z, 1) * 2 + ax, seq)
+        z_across = ((depth - 1 - z) * 2 + ax, seq)
+        stages = 6
+
+        def plan(u, slot, part, peer):
             cp = pltpu.make_async_remote_copy(
-                src_ref=src, dst_ref=w.at[(u, *part)], send_sem=send_sem.at[u, slot], recv_sem=recv_sem.at[u, slot],
-                device_id=peer, device_id_type=MESH)
-            cp.start()
+                src_ref=w.at[(u, *part)], dst_ref=w.at[(u, *part)],
+                send_sem=send_sem.at[u, slot], recv_sem=recv_sem.at[u, slot], device_id=peer, device_id_type=MESH)
             sends[u, slot] = cp
+            return cp
 
         def pass_on(u, slot, part, peer):
-            send(u, slot, w.at[(u, *part)], part, peer)
-
-        for u in range(units):
-            for n in range(hops):
-                pass_on(u, n, (z, ax, y, c), z_peers[n])
-
-        def step_a(u):
-            for n in range(hops):
-                sends[u, n].wait_recv()
-            pass_on(u, B0, (lower, ax, y, c), x_peer)
-            pass_on(u, B1, (upper, ax, y, c), y_peer)
-            pass_on(u, D0, (every, ax, y, c), core_peer)
-
-        def step_b(u):
-            sends[u, B0].wait_recv()
-            pass_on(u, C0, (lower, both, y, c), y_peer)
-            sends[u, B1].wait_recv()
-            pass_on(u, C1, (upper, ax, both, c), x_peer)
-            pass_on(u, D0 + 1, (lower, 1 - ax, y, c), core_peer)
-            pass_on(u, D0 + 2, (upper, ax, 1 - y, c), core_peer)
-
-        def step_c(u):
-            sends[u, C0].wait_recv()
-            pass_on(u, D0 + 3, (lower, both, 1 - y, c), core_peer)
-            sends[u, C1].wait_recv()
-            pass_on(u, D0 + 4, (upper, 1 - ax, both, c), core_peer)
-
-        def step_d(u):
-            for n in range(5):
-                sends[u, D0 + n].wait_recv()
+            plan(u, slot, part, peer).start()
+
+        def from_inner(u, parts):
+            copies = [plan(u, slot, part, peer) for slot, part, peer in parts]
+            for cp, (slot, _, _) in zip(copies, parts):
+                inner_sends.append((u, slot))
+
+            @pl.when(is_inner)
+            def _():
+                for cp in copies:
+                    cp.start()
+
+        def wait_where(here, u, slots):
+            @pl.when(here)
+            def _():
+                for slot in slots:
+                    sends[u, slot].wait_recv()
+
+        def wait_for(u, slots):
+            for slot in slots:
+                sends[u, slot].wait_recv()
+
+        def z_first(u, stage):
+            if stage == 0:
+                pass_on(u, 0, (z, ax, y, c), z_next)
+            elif stage == 1:
+                wait_for(u, (0,))
+                from_inner(u, [(1, (pair, ax, y, c), z_across)])
+            elif stage == 2:
+                wait_where(is_inner, u, (1,))
+                from_inner(u, [(2, (far_pair, ax, y, c), z_next)])
+            elif stage == 3:
+                wait_where(jnp.logical_not(is_inner), u, (2,))
+                pass_on(u, 3, (lower, ax, y, c), x_peer)
+                pass_on(u, 4, (upper, ax, y, c), y_peer)
+                pass_on(u, 7, (every, ax, y, c), core_peer)
+            elif stage == 4:
+                wait_for(u, (3, 4))
+                pass_on(u, 5, (lower, both, y, c), y_peer)
+                pass_on(u, 6, (upper, ax, both, c), x_peer)
+                pass_on(u, 8, (lower, 1 - ax, y, c), core_peer)
+                pass_on(u, 9, (upper, ax, 1 - y, c), core_peer)
+            elif stage == 5:
+                wait_for(u, (5, 6))
+                pass_on(u, 10, (lower, both, 1 - y, c), core_peer)
+                pass_on(u, 11, (upper, 1 - ax, both, c), core_peer)
+            else:
+                wait_for(u, range(7, 12))
+
+        def z_second(u, stage):
+            if stage == 0:
+                pass_on(u, 0, (z, ax, y, c, top), x_peer)
+                pass_on(u, 1, (z, ax, y, c, bottom), y_peer)
+            elif stage == 1:
+                wait_for(u, (0, 1))
+                pass_on(u, 2, (z, both, y, c, top), z_next)
+                pass_on(u, 3, (z, ax, both, c, bottom), z_next)
+            elif stage == 2:
+                wait_for(u, (2, 3))
+                from_inner(u, [(4, (pair, both, y, c, top), z_across), (5, (pair, ax, both, c, bottom), z_across)])
+            elif stage == 3:
+                wait_where(is_inner, u, (4, 5))
+                from_inner(u, [(6, (far_pair, both, y, c, top), z_next), (7, (far_pair, ax, both, c, bottom), z_next)])
+            elif stage == 4:
+                wait_where(jnp.logical_not(is_inner), u, (6, 7))
+                pass_on(u, 8, (every, both, y, c, top), y_peer)
+                pass_on(u, 9, (every, ax, both, c, bottom), x_peer)
+                pass_on(u, 10, (every, both, y, c, top), core_peer)
+                pass_on(u, 11, (every, ax, both, c, bottom), core_peer)
+            elif stage == 5:
+                wait_for(u, (8, 9))
+                pass_on(u, 12, (every, both, 1 - y, c, top), core_peer)
+                pass_on(u, 13, (every, 1 - ax, both, c, bottom), core_peer)
+            else:
+                wait_for(u, range(10, 14))
 
         def arrive(i):
-            if i + 3 < units:
-                step_a(i + 3)
-            if i + 2 < units:
-                step_b(i + 2)
-            if i + 1 < units:
-                step_c(i + 1)
+            for stage in range(stages + 1):
+                u = i + stages - stage
+                if 0 <= u < units:
+                    (z_first if u % 3 == 0 else z_second)(u, stage)
             if i == units - 2:
                 swap_dy.start()
-            step_d(i)
 
         def warm_up():
-            step_a(0)
-            step_a(1)
-            step_b(0)
-            step_a(2)
-            step_b(1)
-            step_c(0)
+            for i in range(-stages, 0):
+                arrive(i)
     else:
         def arrive(i):
             if i == units - 2:
@@ -622,7 +665,13 @@
     for cp in (swap_x, swap_dy, swap_out, swap_dkv, swap_grad):
         cp.wait_send()
     for key in sends:
-        sends[key].wait_send()
+        if key not in inner_sends:
+            sends[key].wait_send()
+    if inner_sends:
+        @pl.when(is_inner)
+        def _():
+            for key in inner_sends:
+                sends[key].wait_send()
 
 
 def whole_step(shards, small, xs, xl, dys, dyl, short_len, long_len, remote):
@@ -633,7 +682,7 @@
     hidden_chunks = small[-1].shape[1] // width
     units = 4 + 2 * hidden_chunks
     lead = (width // CHUNK, 2, 2, 2, CHUNK // 8, width)
-    slots = lead[0] + 8
+    slots = 14
     steps = (dp_size * seq_size).bit_length() - 1
     anywhere = pl.BlockSpec(memory_space=pl.ANY)
     smem = pl.BlockSpec(memory_space=pltpu.SMEM)

time: 221 us -> 213 us (0.964)
  Pallas kernels: 212 us -> 204 us
    pallas_call x1, Pallas kernels: 212 us -> 204 us  [whole_step(): pl.pallas_call(functools.partial(step_kernel, remote, dp_size, seq_size,...]
where the time goes in v5:
time: 213 us; the launch traced here: 212 us
  Pallas kernels  204 us (96%)
  local copies, waits for them, and re-layouts  8.08 us (4%)
    pallas_call x1, Pallas kernels, whole_step(): pl.pallas_call(functools.partial(step_kernel, remote, dp_size, seq_size,...  204 us
    unnamed x13, local copies, waits for them, and re-layouts  6.48 us

profile of v5, /device:TPU:0, one launch (start us, length us, event | category | flops | bytes accessed | tf_op | source)
XLA Modules:
  0.0 212.5 jit_solution(15907743374086080709)
XLA Ops:
  0.7 203.7 %whole_step.1 = (bf16[768,1024]{1,0:T(8,128)(2,1)}, bf16[2,128,1024]{2,1,0:T(8,128)(2,1)}, bf16[768,1024]{1,0:T(8,128)(2,1)}, bf16[2,128,1024]{2,1,0:T(8,128)(2,...) custom-call(f32[32,1024]{1,0:T(8,128)} %refs_0_.1, f32[32,1024]{1,0:T(8,128)} %refs_1_.1, ...), custom_call_target="tpu_custom_call" | custom-call | tf_op jit(solution)/shard_map/whole_step/pallas_call | solution.py:694
  204.4 1.6 fusion
  206.0 0.0 copy-start.2
  206.0 0.0 copy-start
  206.0 2.9 %copy.37 = bf16[6,128,1024]{2,1,0:T(8,128)(2,1)} copy(bf16[6,128,1024]{2,1,0:T(8,128)(2,1)} %bitcast.21) | data formatting | bytes 3145728
  208.9 0.0 copy-done.2
  208.9 0.8 copy.38
  209.7 0.0 copy-done
  209.7 0.0 copy-start.1
  209.7 0.0 copy-start.3
  209.7 1.1 copy.39
  210.9 0.2 copy-done.1
  211.1 0.8 copy.40
  211.9 0.0 copy-done.3
  211.9 0.6 copy.41
Async XLA Ops:
  206.0 2.9 %copy-start.2 = (bf16[2,128,1024]{2,1,0:T(8,128)(2,1)S(1)}, bf16[2,128,1024]{2,1,0:T(8,128)(2,1)}, u32[]{:S(2)}) copy-start(bf16[2,128,1024]{2,1,0:T(8,128)(2,1)} %get-tuple-element.41) | copy-start | bytes 1572868
  206.0 3.7 %copy-start = (bf16[768,1024]{1,0:T(8,128)(2,1)S(1)}, bf16[768,1024]{1,0:T(8,128)(2,1)}, u32[]{:S(2)}) copy-start(bf16[768,1024]{1,0:T(8,128)(2,1)} %get-tuple-element.19) | copy-start | bytes 4718596
  209.7 1.4 copy-start.1
  209.7 2.2 %copy-start.3 = (f32[1,4096]{1,0:T(1,128)S(1)}, f32[1,4096]{1,0:T(1,128)}, u32[]{:S(2)}) copy-start(f32[1,4096]{1,0:T(1,128)} %get-tuple-element.22) | copy-start | bytes 49156

commit v6 on v5

--- a/solution.py
+++ b/solution.py
@@ -23,6 +23,7 @@
 BLOCK = 128
 CHUNK = 256
 TILE = 256
+AHEAD = 3
 K_UNIT, V_UNIT, Q_UNIT, O_UNIT, UP_UNIT = 0, 1, 2, 3, 4
 Q_BIAS, V_BIAS, O_BIAS, D_BIAS, GAIN1, SHIFT1, GAIN2, SHIFT2, U_BIAS = 0, 1, 2, 3, 4, 5, 6, 7, 8
 Q_SUM, V_SUM = 0, 1
@@ -71,7 +72,7 @@
     (xs, xl, dys, dyl, short_len, long_len,
      so, lo, sg, lg, sums, up_sums, parked,
      par, wide_par,
-     w, x, q, k, v, kv_sib, dkv_in, g, r, a16, hid, f, dy, acc, acc_in, tail, tail_in,
+     w, x, q, k, v, kv_sib, dkv_in, g, r, a16, hid, f, dy, acc, acc_in, tail, seq_in, dp_in,
      send_sem, recv_sem, misc_send, misc_recv, own_sem, small_sem, load_sem, store_sem) = refs
     dp = lax.axis_index("dp")
     seq = lax.axis_index("seq")
@@ -102,10 +103,7 @@
 
     if remote:
         z, ax = dp // 2, dp % 2
-        hops = depth - 1
-        z_peers = [((z + n) % depth * 2 + ax, seq) for n in range(1, depth)]
         x_peer = (flipped(dp, 1), seq)
-        peers = z_peers + [x_peer, y_peer, core_peer]
         piece = w.shape[5]
         key_shard, value_shard, query_shard, output_shard, up_shard, down_shard = shards
         sources = [key_shard, value_shard, query_shard, output_shard]
@@ -114,7 +112,6 @@
         own = [pltpu.make_async_copy(source, f.at[pl.ds(n * piece, piece)], own_sem.at[n])
                for n, source in enumerate(sources)]
     else:
-        peers = partners
         own = [pltpu.make_async_copy(shards[0].at[u], w.at[u], own_sem.at[u]) for u in range(units)]
     for cp in own:
         cp.start()
@@ -123,6 +120,9 @@
     for cp in small_loads:
         cp.start()
 
+    seq_peers = [(dp, (seq + n) % seq_size) for n in range(1, seq_size)]
+    dp_peers = [((dp + n) % dp_size, seq) for n in range(1, dp_size)]
+    peers = seq_peers + dp_peers
     barrier = pltpu.get_barrier_semaphore()
     for peer in peers:
         pl.semaphore_signal(barrier, inc=1, device_id=peer, device_id_type=MESH)
@@ -244,25 +244,27 @@
             else:
                 wait_for(u, range(10, 14))
 
+        events = [(i + stages - stage, stage) for i in range(-stages, units) for stage in range(stages + 1)]
+        events = [(u, stage) for u, stage in events if 0 <= u < units]
+
+        def advance(count):
+            for u, stage in events[:count]:
+                (z_first if u % 3 == 0 else z_second)(u, stage)
+                if (u, stage) == (units - 1, stages - 1):
+                    swap_dy.start()
+            del events[:count]
+
         def arrive(i):
-            for stage in range(stages + 1):
-                u = i + stages - stage
-                if 0 <= u < units:
-                    (z_first if u % 3 == 0 else z_second)(u, stage)
-            if i == units - 2:
-                swap_dy.start()
-
-        def warm_up():
-            for i in range(-stages, 0):
-                arrive(i)
+            if (i, stages) in events:
+                advance(events.index((i, stages)) + 1)
     else:
+        def advance(count):
+            pass
+
         def arrive(i):
             if i == units - 2:
                 swap_dy.start()
             own[i].wait()
-
-        def warm_up():
-            pass
 
     def columns(u, at):
         return w[u, :, :, :, :, :, at].reshape(width, CHUNK)
@@ -368,7 +370,7 @@
         acc[0, row : row + 1, at] += row_sum(value)
 
     acc[0] = jnp.zeros_like(acc[0])
-    tail[0] = jnp.zeros_like(tail[0])
+    tail[...] = jnp.zeros_like(tail)
     for cp in small_loads:
         cp.wait()
     for j in range(hidden_chunks):
@@ -378,7 +380,6 @@
             par[U_BIAS + j] = wide_par[:, j * width : (j + 1) * width]
     for cp in loads:
         cp.wait()
-    warm_up()
     arrive(K_UNIT)
     swap_x.wait_recv()
     project(K_UNIT, k, None, None)
@@ -391,34 +392,40 @@
     swap_v.start()
     project(Q_UNIT, q, Q_BIAS, SCALE)
 
-    @phase("sf", 0, nshort // 2)
-    def _(s):
-        short_forward(s)
-
-    arrive(O_UNIT)
-
-    @phase("sf2", nshort // 2, nshort)
-    def _(s):
-        short_forward(s)
-
-    arrive(UP_UNIT)
+    for n in range(3):
+
+        @phase("sf", n * nshort // 3, (n + 1) * nshort // 3)
+        def _(s):
+            short_forward(s)
+
+        if n < 2:
+            advance(AHEAD)
+        else:
+            arrive(O_UNIT)
+
     swap_k.wait_recv()
     swap_v.wait_recv()
-
-    @phase("lf", 0, pairs)
-    def _(h):
-        long_forward(h)
+    for n in range(4):
+
+        @phase("lf", n * pairs // 4, (n + 1) * pairs // 4)
+        def _(h):
+            long_forward(h)
+
+        if n < 3:
+            advance(AHEAD)
 
     swap_k.wait_send()
     swap_v.wait_send()
     park = pltpu.make_async_copy(hid, parked, store_sem.at[4])
     park.start()
-    arrive(UP_UNIT + 1)
+    arrive(UP_UNIT)
 
     @phase("wo", 0, width // CHUNK)
     def _(i):
         at = chunk(i)
         r[:, at] = x[:, at].astype(F32) + dot_nn(g[...], columns(O_UNIT, at)) + par[O_BIAS, :, at]
+
+    advance(AHEAD)
 
     @phase("ln1", 0, total // TILE)
     def _(i):
@@ -431,24 +438,27 @@
     park.wait()
     for j in range(hidden_chunks):
         up, down = UP_UNIT + 2 * j, UP_UNIT + 2 * j + 1
-        if j == 0:
-            arrive(down + 1)
-        elif j > 1:
+        if j > 0:
             arrive(up)
-
-        @phase("up", 0, width // CHUNK)
-        def _(i):
-            at = chunk(i)
-            value = dot_nn(a16[...], columns(up, at)) + par[U_BIAS + j, :, at]
-            active, slope = gelu_parts(value)
-            hid[j, :, at] = slope.astype(BF16)
-            g[:, at] = active.astype(BF16)
+        else:
+            advance(AHEAD)
+        for n in range(2):
+
+            @phase("up", 2 * n, 2 * n + 2)
+            def _(i):
+                at = chunk(i)
+                value = dot_nn(a16[...], columns(up, at)) + par[U_BIAS + j, :, at]
+                active, slope = gelu_parts(value)
+                hid[j, :, at] = slope.astype(BF16)
+                g[:, at] = active.astype(BF16)
+
+            if n == 0:
+                advance(AHEAD)
 
         if j == hidden_chunks - 2:
             for cp in late:
                 cp.start()
-        if j > 0:
-            arrive(down)
+        arrive(down)
 
         @phase("down", 0, width // CHUNK)
         def _(i):
@@ -557,8 +567,8 @@
         v[own_rows, at] = value_grad[: 2 * BLOCK].astype(BF16)
         kv_sib[0, :, at] = key_grad[2 * BLOCK :].astype(BF16)
         kv_sib[1, :, at] = value_grad[2 * BLOCK :].astype(BF16)
-        tail[0, Q_SUM : Q_SUM + 1, at] += query_sum
-        tail[0, V_SUM : V_SUM + 1, at] += row_sum(value_grad)
+        tail[Q_SUM : Q_SUM + 1, at] += query_sum
+        tail[V_SUM : V_SUM + 1, at] += row_sum(value_grad)
 
     def short_backward(s):
         rows = pl.ds(pl.multiple_of(s * BLOCK, BLOCK), BLOCK)
@@ -577,8 +587,8 @@
             q[rows, at] = dq.astype(BF16)
             k[rows, at] = dk.astype(BF16)
             v[rows, at] = dv.astype(BF16)
-            tail[0, Q_SUM : Q_SUM + 1, at] += row_sum(dq)
-            tail[0, V_SUM : V_SUM + 1, at] += row_sum(dv)
+            tail[Q_SUM : Q_SUM + 1, at] += row_sum(dq)
+            tail[V_SUM : V_SUM + 1, at] += row_sum(dv)
 
     next_early(2)
 
@@ -596,23 +606,18 @@
 
     steps = len(partners)
 
-    def late_sum(n):
-        return misc(8 + steps + n, tail.at[n], tail_in.at[n], partners[n])
-
-    def finish_late(n):
-        late_sum(n).wait_recv()
-        late_sum(n).wait_send()
-        tail[n + 1] = tail[n] + tail_in[n]
-
-    def next_late(n):
-        if n > 0:
-            finish_late(n - 1)
-        late_sum(n).start()
-
-    next_late(0)
+    def exchange(slots, me, others, base):
+        return [misc(base + n, slots.at[me], slots.at[me], peer) for n, peer in enumerate(others)]
+
+    seq_round = exchange(seq_in, seq, seq_peers, 8 + steps)
+    dp_round = exchange(dp_in, dp, dp_peers, 8 + steps + len(seq_peers))
+    seq_in[seq] = tail[...]
+
     for n in range(4, steps):
         next_early(n)
     swap_dkv.wait_recv()
+    for cp in seq_round:
+        cp.start()
     k[own_rows, :] = (k[own_rows, :].astype(F32) + dkv_in[0].astype(F32)).astype(BF16)
     v[own_rows, :] = (v[own_rows, :].astype(F32) + dkv_in[1].astype(F32)).astype(BF16)
 
@@ -630,19 +635,23 @@
     swap_grad = misc(6, x.at[pl.ds(short_rows + BLOCK * (1 - y), BLOCK)], lg.at[y], y_peer)
     swap_grad.start()
     finish_early(steps - 1)
-    next_late(1)
+    for cp in seq_round:
+        cp.wait_recv()
+    dp_in[dp] = sum(seq_in[n] for n in range(1, seq_size)) + seq_in[0]
     for i in range(width // CHUNK):
 
         @phase("gxs", i, i + 1)
         def _(n):
             input_grad(pl.ds(0, short_rows), n)
 
-        if i + 2 < steps:
-            next_late(i + 2)
-    for n in range(width // CHUNK + 2, steps):
-        next_late(n)
-    finish_late(steps - 1)
-    sums[0:2, :] = tail[steps]
+        if i == 0:
+            for cp in dp_round:
+                cp.start()
+    for cp in dp_round:
+        cp.wait_recv()
+    for cp in seq_round + dp_round:
+        cp.wait_send()
+    sums[0:2, :] = sum(dp_in[n] for n in range(1, dp_size)) + dp_in[0]
     sums[2:6, :] = acc[steps, 0:4, :]
     hidden_sums = [acc[steps, U_SUM + j : U_SUM + j + 1, :] for j in range(hidden_chunks)]
     if remote:
@@ -684,6 +693,7 @@
     lead = (width // CHUNK, 2, 2, 2, CHUNK // 8, width)
     slots = 14
     steps = (dp_size * seq_size).bit_length() - 1
+    exchanges = 8 + steps + seq_size + dp_size
     anywhere = pl.BlockSpec(memory_space=pl.ANY)
     smem = pl.BlockSpec(memory_space=pltpu.SMEM)
     vmem = pl.BlockSpec(memory_space=pltpu.VMEM)
@@ -713,15 +723,55 @@
             wide, act,
             pltpu.VMEM((steps + 1, 4 + hidden_chunks, width), F32),
             pltpu.VMEM((steps, 4 + hidden_chunks, width), F32),
-            pltpu.VMEM((steps + 1, 2, width), F32),
-            pltpu.VMEM((steps, 2, width), F32),
-            dma((units, slots)), dma((units, slots)), dma((8 + 2 * steps,)), dma((8 + 2 * steps,)),
+            pltpu.VMEM((2, width), F32),
+            pltpu.VMEM((seq_size, 2, width), F32),
+            pltpu.VMEM((dp_size, 2, width), F32),
+            dma((units, slots)), dma((units, slots)), dma((exchanges,)), dma((exchanges,)),
             dma((units,)), dma((len(small),)), dma((4,)), dma((6,)),
         ],
         compiler_params=pltpu.CompilerParams(
             collective_id=0, has_side_effects=True, vmem_limit_bytes=67043328),
         name="whole_step",
     )(*shards, *small, xs, xl, dys, dyl, short_len, long_len)
+
+
+def deliver_kernel(so, lo, sg, lg, sums, up_sums, *refs):
+    outs, deltas = refs[:4], refs[4:11]
+    stages, rows, in_sem, out_sem, row_sem = refs[11:15], refs[15], refs[16], refs[17], refs[18]
+    ins = [pltpu.make_async_copy(ref, stage, in_sem.at[n]) for n, (ref, stage) in enumerate(zip((so, lo, sg, lg), stages))]
+    gather = pltpu.make_async_copy(sums, rows, row_sem.at[0])
+    for cp in ins:
+        cp.start()
+    gather.start()
+    outs = [pltpu.make_async_copy(stage, out, out_sem.at[n]) for n, (stage, out) in enumerate(zip(stages, outs))]
+    gather.wait()
+    for n in range(6):
+        deltas[n][...] = rows[n : n + 1, :]
+    deltas[6][...] = up_sums[...]
+    for n in range(4):
+        ins[n].wait()
+        outs[n].start()
+    for n in range(4):
+        outs[n].wait()
+
+
+def deliver(so, lo, sg, lg, sums, up_sums):
+    anywhere = pl.BlockSpec(memory_space=pl.ANY)
+    vmem = pl.BlockSpec(memory_space=pltpu.VMEM)
+    width = sums.shape[1]
+    big = (so, lo, sg, lg)
+    row = jax.ShapeDtypeStruct((1, width), F32)
+    dma = pltpu.SemaphoreType.DMA
+    return pl.pallas_call(
+        deliver_kernel,
+        out_shape=tuple(jax.ShapeDtypeStruct(a.shape, a.dtype) for a in big)
+        + (row,) * 6 + (jax.ShapeDtypeStruct(up_sums.shape, F32),),
+        in_specs=[anywhere] * 5 + [vmem],
+        out_specs=(anywhere,) * 4 + (vmem,) * 7,
+        scratch_shapes=[pltpu.VMEM(a.shape, a.dtype) for a in big]
+        + [pltpu.VMEM(sums.shape, F32), dma((4,)), dma((4,)), dma((1,))],
+        name="deliver",
+    )(so, lo, sg, lg, sums, up_sums)
 
 
 def on_device(
@@ -758,11 +808,13 @@
         shards, [value.reshape(1, -1) for value in small],
         short_input.reshape(-1, width), long_input, short_cotangent.reshape(-1, width), long_cotangent,
         short_lengths, long_lengths, remote)
+    so, lo, sg, lg, *deltas = deliver(so, lo, sg, lg, sums, up_sums)
+    up_sums = deltas[6]
     if remote:
         upward_delta = up_sums.reshape(-1)
     else:
         upward_delta = jnp.moveaxis(up_sums.reshape(hidden_chunks, devices, rows), 0, 1).reshape(-1)
-    query_delta, value_delta, output_delta, downward_delta, first_delta, second_delta = (sums[n] for n in range(6))
+    query_delta, value_delta, output_delta, downward_delta, first_delta, second_delta = (value.reshape(-1) for value in deltas[:6])
     return (
         so.reshape(shape), lo, sg.reshape(shape), lg,
         query_delta, value_delta, output_delta, upward_delta, downward_delta, first_delta, second_delta,

time: 213 us -> 199 us (0.934)
  local copies, waits for them, and re-layouts: 8.08 us -> 0 us
  Pallas kernels: 204 us -> 198 us
    pallas_call x1, Pallas kernels: 204 us -> 193 us  [whole_step(): pl.pallas_call(functools.partial(step_kernel, remote, dp_size, seq_size,...]
    unnamed x13 -> x0, local copies, waits for them, and re-layouts: 6.48 us -> none
    pallas_call x0 -> x1, Pallas kernels: none -> 4.86 us  [deliver(): pl.pallas_call(deliver_kernel, out_shape=tuple((jax.ShapeDtypeStruct(a.sh...]
where the time goes in v6:
time: 199 us; the launch traced here: 198 us
  Pallas kernels  198 us (99%)
    pallas_call x1, Pallas kernels, whole_step(): pl.pallas_call(functools.partial(step_kernel, remote, dp_size, seq_size,...  193 us
    pallas_call x1, Pallas kernels, deliver(): pl.pallas_call(deliver_kernel, out_shape=tuple((jax.ShapeDtypeStruct(a.sh...  4.86 us

profile of v6, /device:TPU:0, one launch (start us, length us, event | category | flops | bytes accessed | tf_op | source)
XLA Modules:
  0.0 198.3 jit_solution(18036117943674237019)
XLA Ops:
  0.7 192.6 %whole_step.1 = (bf16[768,1024]{1,0:T(8,128)(2,1)}, bf16[2,128,1024]{2,1,0:T(8,128)(2,1)}, bf16[768,1024]{1,0:T(8,128)(2,1)}, bf16[2,128,1024]{2,1,0:T(8,128)(2,...) custom-call(f32[32,1024]{1,0:T(8,128)} %refs_0_.1, f32[32,1024]{1,0:T(8,128)} %refs_1_.1, ...), custom_call_target="tpu_custom_call" | custom-call | tf_op jit(solution)/shard_map/whole_step/pallas_call | solution.py:704
  193.3 4.9 %deliver.1 = (bf16[768,1024]{1,0:T(8,128)(2,1)}, bf16[2,128,1024]{2,1,0:T(8,128)(2,1)}, bf16[768,1024]{1,0:T(8,128)(2,1)}, bf16[2,128,1024]{2,1,0:T(8,128)(2,1)}...) custom-call(bf16[768,1024]{1,0:T(8,128)(2,1)} %get-tuple-element.28., ...), custom_call_target="tpu_custom_call" | custom-call | tf_op jit(solution)/shard_map/deliver/pallas_call | solution.py:765

commit v7 on v6

--- a/solution.py
+++ b/solution.py
@@ -24,6 +24,8 @@
 CHUNK = 256
 TILE = 256
 AHEAD = 3
+Z_FIRST_EVERY = 4
+LEAN_UNIT = -1
 K_UNIT, V_UNIT, Q_UNIT, O_UNIT, UP_UNIT = 0, 1, 2, 3, 4
 Q_BIAS, V_BIAS, O_BIAS, D_BIAS, GAIN1, SHIFT1, GAIN2, SHIFT2, U_BIAS = 0, 1, 2, 3, 4, 5, 6, 7, 8
 Q_SUM, V_SUM = 0, 1
@@ -129,15 +131,13 @@
 
     if remote:
         lanes = width // (8 * depth)
-        for cp in own:
-            cp.wait()
-        for u in range(4):
-            w[u, z, ax, y, c] = f[u * piece : (u + 1) * piece, :].astype(BF16)
-        up_rows = [f[(4 + n) * piece : (5 + n) * piece, :].astype(BF16) for n in range(hidden_chunks)]
-        for j in range(hidden_chunks):
-            first = (4 + hidden_chunks + j) * piece
-            w[UP_UNIT + 2 * j, z, ax, y, c] = jnp.concatenate(every_fourth(up_rows, j, lanes, hidden_chunks), axis=1)
-            w[UP_UNIT + 2 * j + 1, z, ax, y, c] = f[first : first + piece, :].astype(BF16)
+
+        def cast(u, source):
+            own[source].wait()
+            w[u, z, ax, y, c] = f[source * piece : (source + 1) * piece, :].astype(BF16)
+
+        cast(0, 0)
+        cast(1, 1)
     pl.semaphore_wait(barrier, len(peers))
 
     def misc(slot, src, dst, peer):
@@ -218,38 +218,50 @@
                 wait_for(u, range(7, 12))
 
         def z_second(u, stage):
+            own_y = [(1, bottom if u != LEAN_UNIT else pl.ds(0, piece))]
+            ways = own_y if u == LEAN_UNIT else [(0, top)] + own_y
+
+            def slots(first):
+                return [first + way for way, _ in ways]
+
+            def spread(way, at, rows):
+                return (at, both, y, c, rows) if way == 0 else (at, ax, both, c, rows)
+
             if stage == 0:
-                pass_on(u, 0, (z, ax, y, c, top), x_peer)
-                pass_on(u, 1, (z, ax, y, c, bottom), y_peer)
+                for way, rows in ways:
+                    pass_on(u, way, (z, ax, y, c, rows), (x_peer, y_peer)[way])
             elif stage == 1:
-                wait_for(u, (0, 1))
-                pass_on(u, 2, (z, both, y, c, top), z_next)
-                pass_on(u, 3, (z, ax, both, c, bottom), z_next)
+                wait_for(u, slots(0))
+                for way, rows in ways:
+                    pass_on(u, 2 + way, spread(way, z, rows), z_next)
             elif stage == 2:
-                wait_for(u, (2, 3))
-                from_inner(u, [(4, (pair, both, y, c, top), z_across), (5, (pair, ax, both, c, bottom), z_across)])
+                wait_for(u, slots(2))
+                from_inner(u, [(4 + way, spread(way, pair, rows), z_across) for way, rows in ways])
             elif stage == 3:
-                wait_where(is_inner, u, (4, 5))
-                from_inner(u, [(6, (far_pair, both, y, c, top), z_next), (7, (far_pair, ax, both, c, bottom), z_next)])
+                wait_where(is_inner, u, slots(4))
+                from_inner(u, [(6 + way, spread(way, far_pair, rows), z_next) for way, rows in ways])
             elif stage == 4:
-                wait_where(jnp.logical_not(is_inner), u, (6, 7))
-                pass_on(u, 8, (every, both, y, c, top), y_peer)
-                pass_on(u, 9, (every, ax, both, c, bottom), x_peer)
-                pass_on(u, 10, (every, both, y, c, top), core_peer)
-                pass_on(u, 11, (every, ax, both, c, bottom), core_peer)
+                wait_where(jnp.logical_not(is_inner), u, slots(6))
+                for way, rows in ways:
+                    pass_on(u, 8 + way, spread(way, every, rows), (y_peer, x_peer)[way])
+                for way, rows in ways:
+                    pass_on(u, 10 + way, spread(way, every, rows), core_peer)
             elif stage == 5:
-                wait_for(u, (8, 9))
-                pass_on(u, 12, (every, both, 1 - y, c, top), core_peer)
-                pass_on(u, 13, (every, 1 - ax, both, c, bottom), core_peer)
+                wait_for(u, slots(8))
+                for way, rows in ways:
+                    part = (every, both, 1 - y, c, rows) if way == 0 else (every, 1 - ax, both, c, rows)
+                    pass_on(u, 12 + way, part, core_peer)
             else:
-                wait_for(u, range(10, 14))
+                wait_for(u, slots(10) + slots(12))
 
         events = [(i + stages - stage, stage) for i in range(-stages, units) for stage in range(stages + 1)]
         events = [(u, stage) for u, stage in events if 0 <= u < units]
+        events.remove((1, 0))
+        events.insert(1, (1, 0))
 
         def advance(count):
             for u, stage in events[:count]:
-                (z_first if u % 3 == 0 else z_second)(u, stage)
+                (z_first if u % Z_FIRST_EVERY == 0 else z_second)(u, stage)
                 if (u, stage) == (units - 1, stages - 1):
                     swap_dy.start()
             del events[:count]
@@ -271,6 +283,12 @@
 
     def row_block(u, i):
         return w[u, i].reshape(CHUNK, width)
+
+    def row_pair(u, i):
+        return w[u, pl.ds(2 * i, 2)].reshape(2 * CHUNK, width)
+
+    def chunk_pair(i):
+        return pl.ds(pl.multiple_of(i * 2 * CHUNK, 2 * CHUNK), 2 * CHUNK)
 
     def chunk(i):
         return pl.ds(pl.multiple_of(i * CHUNK, CHUNK), CHUNK)
@@ -369,6 +387,16 @@
     def add_sum(row, at, value):
         acc[0, row : row + 1, at] += row_sum(value)
 
+    if remote:
+        advance(2)
+        cast(2, 2)
+        cast(3, 3)
+        for n in range(hidden_chunks):
+            own[4 + n].wait()
+        up_rows = [f[(4 + n) * piece : (5 + n) * piece, :].astype(BF16) for n in range(hidden_chunks)]
+        for j in range(hidden_chunks):
+            w[UP_UNIT + 2 * j, z, ax, y, c] = jnp.concatenate(every_fourth(up_rows, j, lanes, hidden_chunks), axis=1)
+            cast(UP_UNIT + 2 * j + 1, 4 + hidden_chunks + j)
     acc[0] = jnp.zeros_like(acc[0])
     tail[...] = jnp.zeros_like(tail)
     for cp in small_loads:
@@ -490,12 +518,14 @@
     swap_out = misc(4, dy.at[pl.ds(short_rows + BLOCK * (1 - y), BLOCK)], lo.at[y], y_peer)
     swap_out.start()
 
-    @phase("dg", 0, hidden_chunks * (width // CHUNK))
+    pair_count = width // (2 * CHUNK)
+
+    @phase("dg", 0, hidden_chunks * pair_count)
     def _(n):
-        j = n // (width // CHUNK)
-        i = n % (width // CHUNK)
-        at = chunk(i)
-        value = dot_nt(a16[...], row_block(UP_UNIT + 1 + 2 * j, i)) * hid[j, :, at].astype(F32)
+        j = n // pair_count
+        i = n % pair_count
+        at = chunk_pair(i)
+        value = dot_nt(a16[...], row_pair(UP_UNIT + 1 + 2 * j, i)) * hid[j, :, at].astype(F32)
         hid[j, :, at] = value.astype(BF16)
         acc[0, pl.ds(U_SUM + j, 1), at] += row_sum(value)
 

time: 199 us -> 195 us (0.980)
  Pallas kernels: 198 us -> 193 us
    pallas_call x1, Pallas kernels: 193 us -> 189 us  [whole_step(): pl.pallas_call(functools.partial(step_kernel, remote, dp_size, seq_size,...]
where the time goes in v7:
time: 195 us; the launch traced here: 194 us
  Pallas kernels  193 us (99%)
    pallas_call x1, Pallas kernels, whole_step(): pl.pallas_call(functools.partial(step_kernel, remote, dp_size, seq_size,...  189 us
    pallas_call x1, Pallas kernels, deliver(): pl.pallas_call(deliver_kernel, out_shape=tuple((jax.ShapeDtypeStruct(a.sh...  4.86 us

profile of v7, /device:TPU:0, one launch (start us, length us, event | category | flops | bytes accessed | tf_op | source)
XLA Modules:
  0.0 194.3 jit_solution(14646033640297922760)
XLA Ops:
  0.7 188.6 %whole_step.1 = (bf16[768,1024]{1,0:T(8,128)(2,1)}, bf16[2,128,1024]{2,1,0:T(8,128)(2,1)}, bf16[768,1024]{1,0:T(8,128)(2,1)}, bf16[2,128,1024]{2,1,0:T(8,128)(2,...) custom-call(f32[32,1024]{1,0:T(8,128)} %refs_0_.1, f32[32,1024]{1,0:T(8,128)} %refs_1_.1, ...), custom_call_target="tpu_custom_call" | custom-call | tf_op jit(solution)/shard_map/whole_step/pallas_call | solution.py:734
  189.2 4.9 %deliver.1 = (bf16[768,1024]{1,0:T(8,128)(2,1)}, bf16[2,128,1024]{2,1,0:T(8,128)(2,1)}, bf16[768,1024]{1,0:T(8,128)(2,1)}, bf16[2,128,1024]{2,1,0:T(8,128)(2,1)}...) custom-call(bf16[768,1024]{1,0:T(8,128)(2,1)} %get-tuple-element.28., ...), custom_call_target="tpu_custom_call" | custom-call | tf_op jit(solution)/shard_map/deliver/pallas_call | solution.py:795
